TPU v7x, 512 devices: a whole 4x4x16 slice. The times are simulated.
512 devices in a mesh: grp: 64 (over x, z_hi, y), seg: 8 (over z_lo, core).
Axes of the slice: x: 4, y: 4, z: 16 (z_hi: 4, z_lo: 4; z = z_hi * 4 + z_lo), core: 2. Of those that a mesh axis runs over, the one named last changes fastest.
Arguments:
- queries: bfloat16 [524288, 384], P(('grp', 'seg')), may hold values from -16 to 16
- keys: bfloat16 [524288, 384], P(('grp', 'seg')), may hold values from -16 to 16
- values: bfloat16 [524288, 384], P(('grp', 'seg')), may hold values from -6 to 6
Outputs:
- attended: bfloat16 [524288, 384], P(('grp', 'seg'))
All inputs are finite; a program needn't handle non-finite values.
Results may differ from a plain program's by a relative error of at most 0.0041.
Values may be sent and summed in bfloat16 or wider, within the bound.
No kernel may reach another device: no remote copies, remote signals or barrier semaphores. Data moves between devices by JAX's collectives and lax.ppermute only.
A program may use at most 64 MiB of HBM per device.

v0:
```python
import jax
import jax.numpy as jnp
from jax import lax
from jax.sharding import PartitionSpec as P

HEADS = 6
HEAD_WIDTH = 64
SLIDE_GRP = 16


def in_one_piece(arrays, axis, dim, along):
    widths = [a.shape[along] for a in arrays]
    both = jnp.concatenate(arrays, axis=along)
    whole = lax.all_gather(both, axis, axis=dim, tiled=True)
    return tuple(jnp.split(whole, [sum(widths[:k]) for k in range(1, len(widths))], axis=along))


def partner(array, axis, apart):
    return lax.ppermute(array, axis, [(i, i ^ 1 << apart) for i in range(lax.axis_size(axis))])


def attend(query_matrix, key_matrix, value_matrix):
    scores = jnp.einsum(
        "fws,rws->wfr", query_matrix, key_matrix, preferred_element_type=jnp.float32
    ) * HEAD_WIDTH ** (-0.5)
    highest = jnp.max(scores, axis=-1, keepdims=True)
    raised = jnp.exp(scores - highest)
    totals = jnp.sum(raised, axis=-1)
    rounded_length = raised.astype(jnp.bfloat16)
    mixed = (
        jnp.einsum("kgj,jkw->kgw", rounded_length, value_matrix, preferred_element_type=jnp.float32)
        / totals[..., None]
    )
    return (mixed, highest[..., 0] + jnp.log(totals))


def select_rows(source_tensor, period, offsets):
    grouped = source_tensor.reshape(
        source_tensor.shape[0] // period, period, source_tensor.shape[1], source_tensor.shape[2]
    )
    return jnp.stack(
        [grouped[:, offsets[which_head], which_head] for which_head in range(len(offsets))], axis=1
    )


def spread(level_out, level_lse, period, offsets):
    head_total, count, depth = level_out.shape
    marks = (
        jnp.arange(period, dtype=jnp.int32)[None, :] == jnp.array(offsets, dtype=jnp.int32)[:, None]
    )
    cover = jnp.broadcast_to(marks[:, None, :], (head_total, count, period)).reshape(
        head_total, count * period
    )
    out_full = jnp.broadcast_to(
        level_out[:, :, None, :], (head_total, count, period, depth)
    ).reshape(head_total, count * period, depth)
    lse_full = jnp.broadcast_to(level_lse[:, :, None], (head_total, count, period)).reshape(
        head_total, count * period
    )
    return (out_full, lse_full, cover)


def blend(
    near_out,
    near_lse,
    center_output,
    center_logsumexp,
    center_coverage,
    wide_output,
    wide_logsumexp,
    wide_coverage,
):
    mid_level = jnp.where(center_coverage, center_logsumexp, near_lse)
    far_level = jnp.where(wide_coverage, wide_logsumexp, near_lse)
    ceiling = jnp.maximum(jnp.maximum(near_lse, mid_level), far_level)
    near_weight = jnp.exp(near_lse - ceiling)
    mid_weight = jnp.where(center_coverage, jnp.exp(mid_level - ceiling), 0.0)
    far_weight = jnp.where(wide_coverage, jnp.exp(far_level - ceiling), 0.0)
    weighted = (
        near_weight[..., None] * near_out
        + mid_weight[..., None] * center_output
        + far_weight[..., None] * wide_output
    )
    return weighted / (near_weight + mid_weight + far_weight)[..., None]


def body(queries, keys, values):
    row_count = queries.shape[0]
    feature_count = queries.shape[1]
    seg_count = lax.axis_size("seg")
    far_period = SLIDE_GRP * seg_count
    query_split = queries.reshape(row_count, HEADS, HEAD_WIDTH)
    key_split = keys.reshape(row_count, HEADS, HEAD_WIDTH)
    value_split = values.reshape(row_count, HEADS, HEAD_WIDTH)

    def local_head(head_slot):
        start = head_slot * HEAD_WIDTH
        query_cols = lax.dynamic_slice_in_dim(queries, start, HEAD_WIDTH, 1)[:, None, :]
        key_cols = lax.dynamic_slice_in_dim(keys, start, HEAD_WIDTH, 1)[:, None, :]
        value_cols = lax.dynamic_slice_in_dim(values, start, HEAD_WIDTH, 1)[:, None, :]
        mixed, lse_rows = attend(query_cols, key_cols, value_cols)
        return (mixed[0], lse_rows[0])

    near_out, near_lse = lax.map(local_head, jnp.arange(HEADS, dtype=jnp.int32))
    mid_offsets = [which_head % seg_count for which_head in range(HEADS)]
    mid_count = row_count // seg_count
    mid_query = select_rows(query_split, seg_count, mid_offsets)
    mid_key_local = select_rows(key_split, seg_count, mid_offsets).reshape(mid_count, feature_count)
    mid_value_local = select_rows(value_split, seg_count, mid_offsets).reshape(
        mid_count, feature_count
    )
    mid_keys, mid_values = in_one_piece((mid_key_local, mid_value_local), "seg", 0, 1)
    mid_keys = mid_keys.reshape(row_count, HEADS, HEAD_WIDTH)
    mid_values = mid_values.reshape(row_count, HEADS, HEAD_WIDTH)
    center_output, center_logsumexp = attend(mid_query, mid_keys, mid_values)
    far_offsets = [which_head % far_period for which_head in range(HEADS)]
    far_query = select_rows(query_split, far_period, far_offsets)
    far_key_local = select_rows(key_split, far_period, far_offsets).reshape(-1, feature_count)
    far_value_local = select_rows(value_split, far_period, far_offsets).reshape(-1, feature_count)
    far_keys, far_values = in_one_piece((far_key_local, far_value_local), "seg", 0, 1)
    grp_place = lax.axis_index("grp")
    for bit in range(SLIDE_GRP.bit_length() - 1):
        other_keys, other_values = partner((far_keys, far_values), "grp", bit)
        upper_half = grp_place // (1 << bit) % 2 == 1
        far_keys = jnp.where(
            upper_half,
            jnp.concatenate([other_keys, far_keys], axis=0),
            jnp.concatenate([far_keys, other_keys], axis=0),
        )
        far_values = jnp.where(
            upper_half,
            jnp.concatenate([other_values, far_values], axis=0),
            jnp.concatenate([far_values, other_values], axis=0),
        )
    wide_output, wide_logsumexp = attend(
        far_query,
        far_keys.reshape(-1, HEADS, HEAD_WIDTH),
        far_values.reshape(-1, HEADS, HEAD_WIDTH),
    )
    center_output_full, center_logsumexp_full, center_coverage = spread(
        center_output, center_logsumexp, seg_count, mid_offsets
    )
    wide_output_full, wide_logsumexp_full, wide_coverage = spread(
        wide_output, wide_logsumexp, far_period, far_offsets
    )
    combined = blend(
        near_out,
        near_lse,
        center_output_full,
        center_logsumexp_full,
        center_coverage,
        wide_output_full,
        wide_logsumexp_full,
        wide_coverage,
    )
    return combined.transpose(1, 0, 2).reshape(row_count, feature_count).astype(jnp.bfloat16)


def solution(mesh):
    return jax.shard_map(
        body,
        mesh=mesh,
        in_specs=(P(("grp", "seg"), None), P(("grp", "seg"), None), P(("grp", "seg"), None)),
        out_specs=P(("grp", "seg"), None),
        check_vma=False,
    )
```

profile of v0, /device:TPU:48, one launch (start us, length us, event | category | flops | bytes accessed | tf_op | source)
XLA Modules:
  0.0 248.3 jit_solution(11679730896067614773)
XLA Ops:
  11.4 14.8 %all_gather.7 = bf16[64,768]{1,0:T(8,128)(2,1)S(1)} all-gather(bf16[8,768]{1,0:T(8,128)(2,1)S(1)} %pad_maximum_fusion.1), channel_id=1, replica_groups=mesh['grp'=64,'seg'=8] {'seg'}, dimensions={0}, use_global_device_ids=true | all-gather | bytes 110592 | tf_op jit(solution)/shard_map/all_gather | solution.py:14
  26.2 3.2 %collective-permute-start.4 = (bf16[64,384]{1,0:T(8,128)(2,1)S(1)}, bf16[64,384]{1,0:T(8,128)(2,1)S(1)}, u32[]{:S(2)}, u32[]{:S(2)}) collective-permute-start(bf16[64,384]{1,0:T(8,128)(2,1)S(1)} %get-tuple-element.103), channel_id=1, source_target_pairs={{0,8},{8,0},{16,24},{24,16},{32,40},{40,32},{48,56},{56,48},{64,72... | collective-permute-start | bytes 147464 | tf_op jit(solution)/shard_map/ppermute | solution.py:19
  29.4 2.7 %collective-permute-start = (bf16[64,384]{1,0:T(8,128)(2,1)S(1)}, bf16[64,384]{1,0:T(8,128)(2,1)S(1)}, u32[]{:S(2)}, u32[]{:S(2)}) collective-permute-start(bf16[64,384]{1,0:T(8,128)(2,1)S(1)} %get-tuple-element.104), channel_id=1, source_target_pairs={{0,8},{8,0},{16,24},{24,16},{32,40},{40,32},{48,56},{56,48},{64,72... | collective-permute-start | bytes 147464 | tf_op jit(solution)/shard_map/ppermute | solution.py:19
  32.1 2.2 reshape_reshape.19
  34.3 2.1 reshape_reshape.20
  36.4 1.8 fusion.52
  38.8 1.8 fusion.53
  42.5 2.2 reshape_reshape.18
  46.0 35.5 %while.13 = (s32[]{:T(128)}, f32[6,1024,64]{1,2,0:T(8,128)}, f32[6,1024]{1,0:T(8,128)}, s32[6]{0:T(128)S(1)}, bf16[1024,384]{1,0:T(8,128)(2,1)S(1)}, /*index=5*/...) while((s32[]{:T(128)}, f32[6,1024,64]{1,2,0:T(8,128)}, ...), condition=%wide.region_3.4_spmd.clone, body=%wide.region_0.3_spmd.sunk.clone | while | flops 276888576 | bytes 13673635 | solution.py:104
  81.5 1.8 fusion.54
  85.9 2.1 copy.427
  88.1 3.2 %collective-permute-start.5 = (bf16[128,384]{1,0:T(8,128)(2,1)S(1)}, bf16[128,384]{1,0:T(8,128)(2,1)S(1)}, u32[]{:S(2)}, u32[]{:S(2)}) collective-permute-start(bf16[128,384]{1,0:T(8,128)(2,1)S(1)} %maximum_select_fusion.14), channel_id=1, source_target_pairs={{0,16},{8,24},{16,0},{24,8},{32,48},{40,56},{48,32},{56,40},{64,80... | collective-permute-start | bytes 294920 | tf_op jit(solution)/shard_map/ppermute | solution.py:19
  92.6 4.3 %collective-permute-start.1 = (bf16[128,384]{1,0:T(8,128)(2,1)}, bf16[128,384]{1,0:T(8,128)(2,1)S(1)}, u32[]{:S(2)}, u32[]{:S(2)}) collective-permute-start(bf16[128,384]{1,0:T(8,128)(2,1)} %maximum_select_fusion.12), channel_id=1, source_target_pairs={{0,16},{8,24},{16,0},{24,8},{32,48},{40,56},{48,32},{56,40},{64,80... | collective-permute-start | bytes 294920 | tf_op jit(solution)/shard_map/ppermute | solution.py:19
  100.5 9.1 %collective-permute-start.6 = (bf16[256,384]{1,0:T(8,128)(2,1)}, bf16[256,384]{1,0:T(8,128)(2,1)S(1)}, u32[]{:S(2)}, u32[]{:S(2)}) collective-permute-start(bf16[256,384]{1,0:T(8,128)(2,1)} %maximum_select_fusion.10), channel_id=1, source_target_pairs={{0,32},{8,40},{16,48},{24,56},{32,0},{40,8},{48,16},{56,24},{64,96... | collective-permute-start | bytes 589832 | tf_op jit(solution)/shard_map/ppermute | solution.py:19
  110.2 1.7 maximum_select_fusion.8
  111.9 1.9 collective-permute-start.2
  113.9 2.1 maximum_select_fusion.13
  117.6 12.2 %collective-permute-done.6 = bf16[256,384]{1,0:T(8,128)(2,1)S(1)} collective-permute-done((bf16[256,384]{1,0:T(8,128)(2,1)}, bf16[256,384]{1,0:T(8,128)(2,1)S(1)}, u32[]{:S(2)}, u32[]{:S(2)}) %collective-permute-start.6) | collective-permute-done | bytes 196640 | tf_op jit(solution)/shard_map/ppermute | solution.py:19
  129.8 1.9 maximum_select_fusion.6
  131.7 13.3 %collective-permute-start.7 = (bf16[512,384]{1,0:T(8,128)(2,1)}, bf16[512,384]{1,0:T(8,128)(2,1)}, u32[]{:S(2)}, u32[]{:S(2)}) collective-permute-start(bf16[512,384]{1,0:T(8,128)(2,1)} %maximum_select_fusion.6), channel_id=1, source_target_pairs={{0,64},{8,72},{16,80},{24,88},{32,96},{40,104},{48,112},{56,120},{... | collective-permute-start | bytes 1179656 | tf_op jit(solution)/shard_map/ppermute | solution.py:19
  144.9 1.9 maximum_select_fusion.4
  146.9 2.0 collective-permute-start.3
  148.8 1.8 maximum_select_fusion.11
  152.2 1.8 maximum_select_fusion.9
  155.0 2.1 maximum_select_fusion.5
  157.1 1.9 maximum_select_fusion.7
  158.9 46.1 %collective-permute-done.7 = bf16[512,384]{1,0:T(8,128)(2,1)} collective-permute-done((bf16[512,384]{1,0:T(8,128)(2,1)}, bf16[512,384]{1,0:T(8,128)(2,1)}, u32[]{:S(2)}, u32[]{:S(2)}) %collective-permute-start.7) | collective-permute-done | bytes 393248 | tf_op jit(solution)/shard_map/ppermute | solution.py:19
  206.2 10.6 %collective-permute-done.3 = bf16[512,384]{1,0:T(8,128)(2,1)} collective-permute-done((bf16[512,384]{1,0:T(8,128)(2,1)}, bf16[512,384]{1,0:T(8,128)(2,1)}, u32[]{:S(2)}, u32[]{:S(2)}) %collective-permute-start.3) | collective-permute-done | bytes 393248 | tf_op jit(solution)/shard_map/ppermute | solution.py:19
  216.8 1.9 copy.420
  218.7 1.8 fusion.60
  230.1 1.8 reshape.177
  232.7 5.9 %fusion.22 = bf16[6,1024,64]{2,1,0:T(8,128)(2,1)} fusion(f32[6,1024,64]{2,1,0:T(8,128)S(1)} %copy.427, f32[6,1024]{1,0:T(8,128)S(1)} %get-tuple-element.59, f32[6,8,64]{2,1,0:T(8,128)} %convolution_divide_fusion, f32[6,1024]{1,0:T(8,128)S(1)} %get-tuple-element.62, f32[6,128,64]{2,1,0:T(8,128)S(1)} %copy.428, f32[6,1024]{1,0:T(8,128)S(1)} %get-tuple-element.60, ...), kind=kLoop, calls=%fused_computation.19 | loop fusion | flops 2752512 | bytes 2666496 | tf_op jit(solution)/shard_map/convert_element_type | solution.py:156
  (186 shorter events, 66.2 us)
Async XLA Ops:
  6.5 3.0 %copy-start.2 = (bf16[1024,384]{1,0:T(8,128)(2,1)S(1)}, bf16[1024,384]{1,0:T(8,128)(2,1)}, u32[]{:S(2)}) copy-start(bf16[1024,384]{1,0:T(8,128)(2,1)} %param.9) | copy-start | bytes 2359300
  6.5 215.9 %all-gather.2.cloned.1.call-start = ((), (), s32[]{:S(2)}) async-start(), calls=%async_computation | async-start | bytes 1769472 | tf_op jit(solution)/shard_map/all_gather | solution.py:14
  9.1 23.0 %copy-start.1 = (bf16[1024,384]{1,0:T(8,128)(2,1)S(1)}, bf16[1024,384]{1,0:T(8,128)(2,1)}, u32[]{:S(2)}) copy-start(bf16[1024,384]{1,0:T(8,128)(2,1)} %param.8) | copy-start | bytes 2359300
  26.2 61.8 %collective-permute-start.4 = (bf16[64,384]{1,0:T(8,128)(2,1)S(1)}, bf16[64,384]{1,0:T(8,128)(2,1)S(1)}, u32[]{:S(2)}, u32[]{:S(2)}) collective-permute-start(bf16[64,384]{1,0:T(8,128)(2,1)S(1)} %get-tuple-element.103), channel_id=1, source_target_pairs={{0,8},{8,0},{16,24},{24,16},{32,40},{40,32},{48,56},{56,48},{64,72... | collective-permute-start | bytes 147464 | tf_op jit(solution)/shard_map/ppermute | solution.py:19
  29.4 61.9 %collective-permute-start = (bf16[64,384]{1,0:T(8,128)(2,1)S(1)}, bf16[64,384]{1,0:T(8,128)(2,1)S(1)}, u32[]{:S(2)}, u32[]{:S(2)}) collective-permute-start(bf16[64,384]{1,0:T(8,128)(2,1)S(1)} %get-tuple-element.104), channel_id=1, source_target_pairs={{0,8},{8,0},{16,24},{24,16},{32,40},{40,32},{48,56},{56,48},{64,72... | collective-permute-start | bytes 147464 | tf_op jit(solution)/shard_map/ppermute | solution.py:19
  34.3 7.9 %copy-start = (bf16[1024,384]{1,0:T(8,128)(2,1)S(1)}, bf16[1024,384]{1,0:T(8,128)(2,1)}, u32[]{:S(2)}) copy-start(bf16[1024,384]{1,0:T(8,128)(2,1)} %param.7) | copy-start | bytes 2359300
  83.9 2.0 copy-start.9
  84.0 1.6 copy-start.7
  88.1 11.1 %collective-permute-start.5 = (bf16[128,384]{1,0:T(8,128)(2,1)S(1)}, bf16[128,384]{1,0:T(8,128)(2,1)S(1)}, u32[]{:S(2)}, u32[]{:S(2)}) collective-permute-start(bf16[128,384]{1,0:T(8,128)(2,1)S(1)} %maximum_select_fusion.14), channel_id=1, source_target_pairs={{0,16},{8,24},{16,0},{24,8},{32,48},{40,56},{48,32},{56,40},{64,80... | collective-permute-start | bytes 294920 | tf_op jit(solution)/shard_map/ppermute | solution.py:19
  91.3 0.6 copy-start.6
  92.6 17.0 %collective-permute-start.1 = (bf16[128,384]{1,0:T(8,128)(2,1)}, bf16[128,384]{1,0:T(8,128)(2,1)S(1)}, u32[]{:S(2)}, u32[]{:S(2)}) collective-permute-start(bf16[128,384]{1,0:T(8,128)(2,1)} %maximum_select_fusion.12), channel_id=1, source_target_pairs={{0,16},{8,24},{16,0},{24,8},{32,48},{40,56},{48,32},{56,40},{64,80... | collective-permute-start | bytes 294920 | tf_op jit(solution)/shard_map/ppermute | solution.py:19
  99.2 0.6 copy-start.4
  100.5 29.3 %collective-permute-start.6 = (bf16[256,384]{1,0:T(8,128)(2,1)}, bf16[256,384]{1,0:T(8,128)(2,1)S(1)}, u32[]{:S(2)}, u32[]{:S(2)}) collective-permute-start(bf16[256,384]{1,0:T(8,128)(2,1)} %maximum_select_fusion.10), channel_id=1, source_target_pairs={{0,32},{8,40},{16,48},{24,56},{32,0},{40,8},{48,16},{56,24},{64,96... | collective-permute-start | bytes 589832 | tf_op jit(solution)/shard_map/ppermute | solution.py:19
  109.6 0.6 copy-start.3
  111.9 33.0 %collective-permute-start.2 = (bf16[256,384]{1,0:T(8,128)(2,1)}, bf16[256,384]{1,0:T(8,128)(2,1)S(1)}, u32[]{:S(2)}, u32[]{:S(2)}) collective-permute-start(bf16[256,384]{1,0:T(8,128)(2,1)} %maximum_select_fusion.8), channel_id=1, source_target_pairs={{0,32},{8,40},{16,48},{24,56},{32,0},{40,8},{48,16},{56,24},{64,96... | collective-permute-start | bytes 589832 | tf_op jit(solution)/shard_map/ppermute | solution.py:19
  131.7 73.4 %collective-permute-start.7 = (bf16[512,384]{1,0:T(8,128)(2,1)}, bf16[512,384]{1,0:T(8,128)(2,1)}, u32[]{:S(2)}, u32[]{:S(2)}) collective-permute-start(bf16[512,384]{1,0:T(8,128)(2,1)} %maximum_select_fusion.6), channel_id=1, source_target_pairs={{0,64},{8,72},{16,80},{24,88},{32,96},{40,104},{48,112},{56,120},{... | collective-permute-start | bytes 1179656 | tf_op jit(solution)/shard_map/ppermute | solution.py:19
  146.9 70.0 %collective-permute-start.3 = (bf16[512,384]{1,0:T(8,128)(2,1)}, bf16[512,384]{1,0:T(8,128)(2,1)}, u32[]{:S(2)}, u32[]{:S(2)}) collective-permute-start(bf16[512,384]{1,0:T(8,128)(2,1)} %maximum_select_fusion.4), channel_id=1, source_target_pairs={{0,64},{8,72},{16,80},{24,88},{32,96},{40,104},{48,112},{56,120},{... | collective-permute-start | bytes 1179656 | tf_op jit(solution)/shard_map/ppermute | solution.py:19
  218.7 2.7 %copy-start.5 = (bf16[512,6,64]{0,2,1:T(8,128)(2,1)S(1)}, bf16[512,6,64]{0,2,1:T(8,128)(2,1)}, u32[]{:S(2)}) copy-start(bf16[512,6,64]{0,2,1:T(8,128)(2,1)} %maximum_select_fusion.7) | copy-start | bytes 1179652
  222.4 1.5 copy-start.8
Sparse Core Ops, SparseCore 0:
  42.2 41.8 all-gather.1
where the time goes:
time: 250 us; the launch traced here: 248 us
  waiting for transfers between devices  69 us (28%)
  local copies, waits for them, and re-layouts  57.4 us (23%)
  starting transfers between devices  39.6 us (16%)
  other arithmetic  29.8 us (12%)
  matrix products  19.4 us (8%)
  blocking collectives  14.8 us (6%)
  between operations  14.1 us (6%)
  loops' own time  4.25 us (2%)
    ppermute x8, waiting for transfers between devices, partner(): lax.ppermute(array, axis, [(i, i ^ 1 << apart) for i in range(lax.axis_si...  68.9 us
    ppermute x8, starting transfers between devices, partner(): lax.ppermute(array, axis, [(i, i ^ 1 << apart) for i in range(lax.axis_si...  39.5 us
    all_gather x1, blocking collectives, in_one_piece(): whole = lax.all_gather(both, axis, axis=dim, tiled=True)  14.8 us
    dot_general x8, matrix products, attend(): jnp.einsum('kgj,jkw->kgw', rounded_length, value_matrix, preferred_elemen...  12.1 us
    select_n x6, other arithmetic, body(): jnp.where(upper_half, jnp.concatenate([other_keys, far_keys], axis=0), jn...  10.2 us
    slice x30, local copies, waits for them, and re-layouts, select_rows(): grouped[:, offsets[which_head], which_head]  9.16 us
    dynamic_update_slice x6, local copies, waits for them, and re-layouts, body(): near_out, near_lse = lax.map(local_head, jnp.arange(HEADS, dtype=jnp.int32))  8.33 us
    ppermute x6, local copies, waits for them, and re-layouts, partner(): lax.ppermute(array, axis, [(i, i ^ 1 << apart) for i in range(lax.axis_si...  7.32 us
  transfers between devices with their start and end apart: 9, of which 3 were waited for; matrix products, arithmetic and copies ran while one was open for 33% of the time, Pallas kernels for 0%

commit v1 on v0

v1 whole, which is shorter than its diff:
```python
import jax
import jax.numpy as jnp
from jax import lax
from jax.experimental import pallas as pl
from jax.experimental.pallas import tpu as pltpu
from jax.sharding import PartitionSpec as P

HEADS = 6
HEAD_WIDTH = 64
PAIRS = HEADS // 2
LANES = 2 * HEAD_WIDTH
SLIDE_GRP = 16
SEG = 8
ROWS = 1024
MID = ROWS // SEG
FAR_PERIOD = SLIDE_GRP * SEG
FAR = ROWS // FAR_PERIOD
CHUNK = 256
SCALE = HEAD_WIDTH ** (-0.5)


NT = (((1,), (1,)), ((), ()))
NN = (((1,), (0,)), ((), ()))
TN = (((0,), (0,)), ((), ()))
F32 = jnp.float32
BF16 = jnp.bfloat16

SEND_MID = 224
BACK_MID = 80
BACK = BACK_MID + (PAIRS + 1) * FAR


def dot(a, b, dims):
    return lax.dot_general(a, b, dims, preferred_element_type=F32)


def lane_low(shape):
    return lax.broadcasted_iota(jnp.int32, shape, len(shape) - 1) < HEAD_WIDTH


def split3(x):
    high = x.astype(BF16)
    rest = x - high.astype(F32)
    middle = rest.astype(BF16)
    low = (rest - middle.astype(F32)).astype(BF16)
    return high, middle, low


def pack_kernel(q_ref, k_ref, v_ref, mid_ref, far_ref, q_wide, k_wide, v_wide):
    far_q, far_k, far_v = [], [], []
    low_mid = lane_low((MID, LANES))
    low_half = lane_low((MID // 2, LANES))
    low_far = lane_low((FAR, LANES))
    for pair in range(PAIRS):
        cols = slice(pair * LANES, (pair + 1) * LANES)
        q_wide[...] = q_ref[:, cols].astype(F32)
        k_wide[...] = k_ref[:, cols].astype(F32)
        v_wide[...] = v_ref[:, cols].astype(F32)
        for side in range(2):
            head = 2 * pair + side
            q_rows = q_wide[pl.ds(head, MID, stride=SEG), :]
            k_rows = k_wide[pl.ds(head, MID, stride=SEG), :]
            v_rows = v_wide[pl.ds(head, MID, stride=SEG), :]
            if side == 0:
                key_value = jnp.where(low_mid, k_rows, pltpu.roll(v_rows, HEAD_WIDTH, 1))
                query = jnp.where(
                    low_half, q_rows[: MID // 2], pltpu.roll(q_rows[MID // 2 :], HEAD_WIDTH, 1)
                )
            else:
                key_value = jnp.where(low_mid, pltpu.roll(k_rows, HEAD_WIDTH, 1), v_rows)
                query = jnp.where(
                    low_half, pltpu.roll(q_rows[: MID // 2], HEAD_WIDTH, 1), q_rows[MID // 2 :]
                )
            mid_ref[head, 0:MID, :] = key_value.astype(BF16)
            mid_ref[head, MID : MID + MID // 2, :] = query.astype(BF16)
        for wide, out in ((q_wide, far_q), (k_wide, far_k), (v_wide, far_v)):
            first = wide[pl.ds(2 * pair, FAR, stride=FAR_PERIOD), :]
            second = wide[pl.ds(2 * pair + 1, FAR, stride=FAR_PERIOD), :]
            out.append(jnp.where(low_far, first, second))
    for spare in range(HEADS, SEG):
        mid_ref[spare, 0 : MID + MID // 2, :] = jnp.zeros((MID + MID // 2, LANES), BF16)
    tail = jnp.concatenate(far_q + [jnp.zeros((FAR, LANES), F32)], axis=0).astype(BF16)
    for target in range(SEG):
        mid_ref[target, MID + MID // 2 : SEND_MID, :] = tail
    both = jnp.concatenate(far_k + far_v, axis=0).astype(BF16)
    for target in range(SLIDE_GRP):
        far_ref[target] = both


def pack(queries, keys, values):
    return pl.pallas_call(
        pack_kernel,
        out_shape=(
            jax.ShapeDtypeStruct((SEG, SEND_MID, LANES), BF16),
            jax.ShapeDtypeStruct((SLIDE_GRP, 2 * PAIRS * FAR, LANES), BF16),
        ),
        scratch_shapes=[pltpu.VMEM((ROWS, LANES), F32)] * 3,
        name="pack",
    )(queries, keys, values)


def scores_of(key_rows, query_rows):
    return dot(key_rows, query_rows, NT)


def finish(scores, value_columns):
    highest = jnp.max(scores, axis=0, keepdims=True)
    raised = jnp.exp(scores - highest).astype(BF16)
    mixed = dot(value_columns, raised, NN)
    totals = mixed[HEAD_WIDTH : HEAD_WIDTH + 1]
    return mixed[:HEAD_WIDTH] / totals, highest + jnp.log(totals)


def chunks_of(key_rows, query_parts, value_parts, put):
    count = len(query_parts)
    pending = scores_of(key_rows, query_parts[0]())
    for step in range(count):
        following = scores_of(key_rows, query_parts[step + 1]()) if step + 1 < count else None
        mixed, lse = finish(pending, value_parts[step])
        put(step, mixed, lse)
        pending = following


def near_kernel(q_ref, k_ref, v_ref, o_ref, l_ref):
    key_rows = k_ref[...]
    columns = v_ref[...].T
    ones = jnp.ones((16, ROWS), BF16)
    sides = [
        jnp.concatenate([columns[i * HEAD_WIDTH : (i + 1) * HEAD_WIDTH], ones], axis=0)
        for i in range(2)
    ]
    low = lane_low((CHUNK, LANES))
    per_side = ROWS // CHUNK

    def query_part(side, part):
        def get():
            rows = q_ref[part * CHUNK : (part + 1) * CHUNK, :] * BF16(SCALE)
            keep = low if side == 0 else jnp.logical_not(low)
            return jnp.where(keep, rows, BF16(0))

        return get

    def put(step, mixed, lse):
        side, part = step // per_side, step % per_side
        span = slice(part * CHUNK, (part + 1) * CHUNK)
        o_ref[side * HEAD_WIDTH : (side + 1) * HEAD_WIDTH, span] = mixed.astype(BF16)
        l_ref[0, side : side + 1, span] = lse

    chunks_of(
        key_rows,
        [query_part(s, p) for s in range(2) for p in range(per_side)],
        [sides[s] for s in range(2) for _ in range(per_side)],
        put,
    )


def near(queries, keys, values, first, count):
    spec = pl.BlockSpec((ROWS, LANES), lambda i: (0, i + first))
    return pl.pallas_call(
        near_kernel,
        grid=(count,),
        in_specs=[spec] * 3,
        out_specs=(
            pl.BlockSpec((LANES, ROWS), lambda i: (i, 0)),
            pl.BlockSpec((1, 8, ROWS), lambda i: (i, 0, 0)),
        ),
        out_shape=(
            jax.ShapeDtypeStruct((count * LANES, ROWS), BF16),
            jax.ShapeDtypeStruct((count, 8, ROWS), F32),
        ),
        cost_estimate=pl.CostEstimate(
            flops=count * 2 * 4 * ROWS * ROWS * HEAD_WIDTH,
            bytes_accessed=count * 4 * ROWS * LANES * 2,
            transcendentals=count * 2 * ROWS * ROWS,
        ),
        name="near",
    )(queries, keys, values)


def mid_kernel(r_ref, s_ref):
    key_value = r_ref[:, 0:MID, :].reshape(ROWS, LANES)
    columns = jnp.concatenate(
        [key_value.T[HEAD_WIDTH:], jnp.ones((16, ROWS), BF16)], axis=0
    )
    low = lane_low((MID // 2, LANES))

    def query_block(source):
        packed = r_ref[source, MID : MID + MID // 2, :].astype(F32) * SCALE
        first = jnp.where(low, packed, 0.0)
        second = jnp.where(low, pltpu.roll(packed, HEAD_WIDTH, 1), 0.0)
        return jnp.concatenate([first, second], axis=0).astype(BF16)

    def query_part(step):
        return lambda: jnp.concatenate([query_block(2 * step), query_block(2 * step + 1)], axis=0)

    def put(step, mixed, lse):
        parts = [part.astype(F32) for part in split3(lse)]
        block = jnp.concatenate(
            [mixed] + parts + [jnp.zeros((BACK_MID - HEAD_WIDTH - 3, CHUNK), F32)], axis=0
        ).astype(BF16)
        s_ref[2 * step] = block[:, :MID]
        s_ref[2 * step + 1] = block[:, MID:]

    steps = ROWS // CHUNK
    chunks_of(key_value, [query_part(s) for s in range(steps)], [columns] * steps, put)


def mid(received):
    return pl.pallas_call(
        mid_kernel,
        out_shape=jax.ShapeDtypeStruct((SEG, BACK_MID, MID), BF16),
        cost_estimate=pl.CostEstimate(
            flops=4 * ROWS * ROWS * HEAD_WIDTH,
            bytes_accessed=ROWS * LANES * 4,
            transcendentals=ROWS * ROWS,
        ),
        name="mid",
    )(received)


def far_kernel(r_ref, f_ref, m_ref, s_ref):
    queries = r_ref[:, MID + MID // 2 : SEND_MID, :].astype(F32) * SCALE
    others = f_ref[...].astype(F32)
    count = SEG * FAR
    low = lane_low((count, LANES))
    lane = lax.broadcasted_iota(jnp.int32, (count, LANES), 1)
    marks = jnp.zeros((count, LANES), F32)
    pieces = []
    for pair in range(PAIRS):
        rows = queries[:, pair * FAR : (pair + 1) * FAR, :].reshape(count, LANES)
        key_rows = (
            others[:, pair * FAR : (pair + 1) * FAR, :].reshape(SLIDE_GRP * FAR, LANES).astype(BF16)
        )
        value_rows = (
            others[:, (PAIRS + pair) * FAR : (PAIRS + pair + 1) * FAR, :]
            .reshape(SLIDE_GRP * FAR, LANES)
            .astype(BF16)
        )
        outs = []
        for side in range(2):
            keep = low if side == 0 else jnp.logical_not(low)
            scores = dot(jnp.where(keep, rows, 0.0).astype(BF16), key_rows, NT)
            highest = jnp.max(scores, axis=1, keepdims=True)
            raised = jnp.exp(scores - highest)
            totals = jnp.sum(raised, axis=1, keepdims=True)
            outs.append(dot(raised.astype(BF16), value_rows, NN) / totals)
            for place, part in enumerate(split3(highest + jnp.log(totals))):
                marks = jnp.where(
                    lane == 3 * (2 * pair + side) + place, part.astype(F32), marks
                )
        pieces.append(jnp.where(low, outs[0], outs[1]).reshape(SEG, FAR, LANES))
    pieces.append(marks.reshape(SEG, FAR, LANES))
    s_ref[:, BACK_MID:, :] = jnp.concatenate(pieces, axis=1).astype(BF16)
    s_ref[:, :BACK_MID, :] = m_ref[...]


def far(received, others, mid_part):
    return pl.pallas_call(
        far_kernel,
        out_shape=jax.ShapeDtypeStruct((SEG, BACK, LANES), BF16),
        name="far",
    )(received, others, mid_part)


def merge_kernel(*refs):
    n = (len(refs) - 2) // 2
    near_refs, lse_refs = refs[:n], refs[n : 2 * n]
    back_ref, out_ref = refs[2 * n :]
    width = HEADS * HEAD_WIDTH
    parts = back_ref[:, BACK_MID:, :].astype(F32)
    count = SEG * FAR
    marks = parts[:, PAIRS * FAR :, :].reshape(count, LANES).astype(BF16)
    source = lax.broadcasted_iota(jnp.int32, (LANES, width), 0)
    target = lax.broadcasted_iota(jnp.int32, (LANES, width), 1) // HEAD_WIDTH
    gather = jnp.logical_and(source >= 3 * target, source < 3 * target + 3).astype(BF16)
    lse_parts = dot(marks, gather, NN).reshape(SEG, FAR, width)
    far_parts = jnp.concatenate(
        [
            parts[:, pair * FAR : (pair + 1) * FAR, :].reshape(count, LANES)
            for pair in range(PAIRS)
        ],
        axis=1,
    ).reshape(SEG, FAR, width)
    top = jnp.max(lse_parts, axis=0)
    weights = jnp.exp(lse_parts - top[None])
    total = jnp.sum(weights, axis=0)
    far_out = jnp.sum(weights * far_parts, axis=0) / total
    far_lse = top + jnp.log(total)
    place = lax.broadcasted_iota(jnp.int32, (FAR, MID), 0) * (MID // FAR)
    lane = lax.broadcasted_iota(jnp.int32, (FAR, MID), 1)
    thin = (lane == place).astype(BF16)
    far_rows = jnp.concatenate([far_out] + [x.astype(F32) for x in split3(far_lse)], axis=1)
    far_wide = dot(far_rows.astype(BF16), thin, TN)
    has_far = lax.broadcasted_iota(jnp.int32, (1, MID), 1) % (MID // FAR) == 0
    slot = lax.broadcasted_iota(jnp.int32, (MID, ROWS), 0) * SEG
    token = lax.broadcasted_iota(jnp.int32, (MID, ROWS), 1)
    offset = token - slot
    phase = lax.broadcasted_iota(jnp.int32, (1, ROWS), 1) % SEG
    start = 0
    for ref, lse_ref in zip(near_refs, lse_refs):
        for pair in range(ref.shape[0] // LANES):
            sides = []
            for side in range(2):
                head = start + 2 * pair + side
                back = back_ref[head, :BACK_MID].astype(F32)
                mid_out = back[:HEAD_WIDTH]
                mid_lse = back[64:65] + back[65:66] + back[66:67]
                base = head * HEAD_WIDTH
                w_out = far_wide[base : base + HEAD_WIDTH]
                w_lse = (
                    far_wide[width + base : width + base + 1]
                    + far_wide[2 * width + base : 2 * width + base + 1]
                    + far_wide[3 * width + base : 3 * width + base + 1]
                )
                w_lse = jnp.where(has_far, w_lse, mid_lse)
                high = jnp.maximum(mid_lse, w_lse)
                w_mid = jnp.exp(mid_lse - high)
                w_far = jnp.where(has_far, jnp.exp(w_lse - high), 0.0)
                sums = w_mid + w_far
                joint = (w_mid * mid_out + w_far * w_out) / sums
                joint_lse = high + jnp.log(sums)
                block = jnp.concatenate(
                    [joint]
                    + [x.astype(F32) for x in split3(joint_lse)]
                    + [jnp.zeros((BACK_MID - HEAD_WIDTH - 3, MID), F32)],
                    axis=0,
                ).astype(BF16)
                spread = dot(block, (offset == head).astype(BF16), NN)
                near_lse = lse_ref[pair, side : side + 1, :]
                joint_wide = spread[64:65] + spread[65:66] + spread[66:67]
                covered = phase == head
                joint_wide = jnp.where(covered, joint_wide, near_lse)
                ceiling = jnp.maximum(near_lse, joint_wide)
                near_weight = jnp.exp(near_lse - ceiling)
                joint_weight = jnp.where(covered, jnp.exp(joint_wide - ceiling), 0.0)
                share = joint_weight / (near_weight + joint_weight)
                rest = near_weight / (near_weight + joint_weight)
                own = ref[
                    pair * LANES + side * HEAD_WIDTH : pair * LANES + (side + 1) * HEAD_WIDTH, :
                ].astype(F32)
                sides.append(rest * own + share * spread[:HEAD_WIDTH])
            whole = start // 2 + pair
            out_ref[:, whole * LANES : (whole + 1) * LANES] = (
                jnp.concatenate(sides, axis=0).astype(BF16).T
            )
        start += 2 * (ref.shape[0] // LANES)


def merge(near_outs, near_lses, back):
    return pl.pallas_call(
        merge_kernel,
        out_shape=jax.ShapeDtypeStruct((ROWS, HEADS * HEAD_WIDTH), BF16),
        name="merge",
    )(*near_outs, *near_lses, back)


def body(queries, keys, values):
    groups = lax.axis_size("grp") // SLIDE_GRP
    slides = [[s * SLIDE_GRP + i for i in range(SLIDE_GRP)] for s in range(groups)]
    mid_send, far_send = pack(queries, keys, values)
    mid_got = lax.all_to_all(mid_send, "seg", 0, 0, tiled=True)
    far_got = lax.all_to_all(
        far_send, "grp", 0, 0, tiled=True, axis_index_groups=slides
    )
    nears = []
    for pair in range(3):
        nears.append(near(queries, keys, values, pair, 1))
    mid_part = mid(mid_got)
    part = far(mid_got, far_got, mid_part)
    back = lax.all_to_all(part, "seg", 0, 0, tiled=True)
    return merge([n[0] for n in nears], [n[1] for n in nears], back)


def solution(mesh):
    return jax.shard_map(
        body,
        mesh=mesh,
        in_specs=(P(("grp", "seg"), None),) * 3,
        out_specs=P(("grp", "seg"), None),
        check_vma=False,
    )
```

time: 250 us -> 86.9 us (0.35)
  the two profiles are of different devices: /device:TPU:48 before, /device:TPU:1 now
where the time goes in v1:
time: 86.9 us; the launch traced here: 86.4 us
  Pallas kernels  29.7 us (34%)
  blocking collectives  23.9 us (28%)
  starting transfers between devices  20.3 us (23%)
  waiting for transfers between devices  11.1 us (13%)
  local copies, waits for them, and re-layouts  1.35 us (2%)
    all_to_all x1, blocking collectives, body(): mid_got = lax.all_to_all(mid_send, 'seg', 0, 0, tiled=True)  23.9 us
    pallas_call x3, Pallas kernels, near(): pl.pallas_call(near_kernel, grid=(count,), in_specs=[spec] * 3, out_specs...  16.4 us
    all_to_all x1, starting transfers between devices, body(): lax.all_to_all(far_send, 'grp', 0, 0, tiled=True, axis_index_groups=slides)  12.2 us
    all_to_all x1, waiting for transfers between devices, body(): lax.all_to_all(far_send, 'grp', 0, 0, tiled=True, axis_index_groups=slides)  11.1 us
    all_to_all x1, starting transfers between devices, body(): back = lax.all_to_all(part, 'seg', 0, 0, tiled=True)  8.06 us
    pallas_call x1, Pallas kernels, mid(): pl.pallas_call(mid_kernel, out_shape=jax.ShapeDtypeStruct((SEG, BACK_MID,...  3.63 us
    pallas_call x1, Pallas kernels, merge(): pl.pallas_call(merge_kernel, out_shape=jax.ShapeDtypeStruct((ROWS, HEADS...  3.38 us
    pallas_call x1, Pallas kernels, far(): pl.pallas_call(far_kernel, out_shape=jax.ShapeDtypeStruct((SEG, BACK, LAN...  3.37 us
  transfers between devices with their start and end apart: 2, of which 1 were waited for; matrix products, arithmetic and copies ran while one was open for 0% of the time, Pallas kernels for 23%

profile of v1, /device:TPU:1, one launch (start us, length us, event | category | flops | bytes accessed | tf_op | source)
XLA Modules:
  0.0 86.4 jit_solution(17317179569826997665)
XLA Ops:
  0.0 3.0 %pack.1 = (bf16[8,224,128]{2,1,0:T(8,128)(2,1)}, bf16[16,48,128]{2,1,0:T(8,128)(2,1)}) custom-call(bf16[1024,384]{1,0:T(8,128)(2,1)} %q_ref.7, bf16[1024,384]{1,0:T(8,128)(2,1)} %k_ref.7, bf16[1024,384]{1,0:T(8,128)(2,1)} %v_ref.7), custom_call_target="tpu_custom_call" | custom-call | tf_op jit(solution)/shard_map/pack/pallas_call | solution.py:91
  3.0 23.9 %all_to_all.15.r_ref = bf16[8,224,128]{2,1,0:T(8,128)(2,1)} all-to-all(bf16[8,224,128]{2,1,0:T(8,128)(2,1)} %get-tuple-element.19), channel_id=1, replica_groups=mesh['grp'=64,'seg'=8] {'seg'}, dimensions={0} | all-to-all | bytes 917504 | tf_op jit(solution)/shard_map/all_to_all | solution.py:361
  26.9 12.2 %all-to-all-start.1 = ((bf16[16,48,128]{2,1,0:T(8,128)(2,1)}), bf16[16,48,128]{2,1,0:T(8,128)(2,1)S(1)}, u32[]{:S(2)}, u32[]{:S(2)}) async-start(bf16[16,48,128]{2,1,0:T(8,128)(2,1)} %get-tuple-element.20), calls=%async_computation.1 | async-start | bytes 393216 | tf_op jit(solution)/shard_map/all_to_all | solution.py:362
  39.1 3.6 %mid.1.m_ref = bf16[8,80,128]{2,1,0:T(8,128)(2,1)} custom-call(bf16[8,224,128]{2,1,0:T(8,128)(2,1)} %all_to_all.15.r_ref), custom_call_target="tpu_custom_call" | custom-call | flops 268435456 | bytes 524288 | tf_op jit(solution)/shard_map/mid/pallas_call | solution.py:209
  42.7 11.1 %all-to-all-done.1.f_ref = bf16[16,48,128]{2,1,0:T(8,128)(2,1)S(1)} async-done(((bf16[16,48,128]{2,1,0:T(8,128)(2,1)}), bf16[16,48,128]{2,1,0:T(8,128)(2,1)S(1)}, u32[]{:S(2)}, u32[]{:S(2)}) %all-to-all-start.1) | async-done | bytes 196640 | tf_op jit(solution)/shard_map/all_to_all | solution.py:362
  53.8 0.0 copy-start.1
  53.8 0.7 copy-done.1
  54.5 3.4 %far.1 = bf16[8,112,128]{2,1,0:T(8,128)(2,1)} custom-call(bf16[8,224,128]{2,1,0:T(8,128)(2,1)} %all_to_all.15.r_ref, bf16[16,48,128]{2,1,0:T(8,128)(2,1)} %copy-done.1, bf16[8,80,128]{2,1,0:T(8,128)(2,1)} %mid.1.m_ref), custom_call_target="tpu_custom_call" | custom-call | tf_op jit(solution)/shard_map/far/pallas_call | solution.py:258
  57.9 8.1 %all-to-all-start.2 = ((bf16[8,112,128]{2,1,0:T(8,128)(2,1)}), bf16[8,112,128]{2,1,0:T(8,128)(2,1)S(1)}, u32[]{:S(2)}, u32[]{:S(2)}) async-start(bf16[8,112,128]{2,1,0:T(8,128)(2,1)} %far.1), calls=%async_computation.2 | async-start | bytes 458752 | tf_op jit(solution)/shard_map/all_to_all | solution.py:370
  65.9 5.5 %near.3 = (bf16[128,1024]{1,0:T(8,128)(2,1)}, f32[1,8,1024]{2,1,0:T(8,128)}) custom-call(bf16[1024,384]{1,0:T(8,128)(2,1)} %q_ref.7, bf16[1024,384]{1,0:T(8,128)(2,1)} %k_ref.7, bf16[1024,384]{1,0:T(8,128)(2,1)} %v_ref.7), custom_call_target="tpu_custom_call" | custom-call | flops 536870912 | bytes 1048576 | tf_op jit(solution)/shard_map/near/pallas_call | solution.py:159
  71.4 5.5 %near.4 = (bf16[128,1024]{1,0:T(8,128)(2,1)}, f32[1,8,1024]{2,1,0:T(8,128)}) custom-call(bf16[1024,384]{1,0:T(8,128)(2,1)} %q_ref.7, bf16[1024,384]{1,0:T(8,128)(2,1)} %k_ref.7, bf16[1024,384]{1,0:T(8,128)(2,1)} %v_ref.7), custom_call_target="tpu_custom_call" | custom-call | flops 536870912 | bytes 1048576 | tf_op jit(solution)/shard_map/near/pallas_call | solution.py:159
  76.8 5.5 %near.5 = (bf16[128,1024]{1,0:T(8,128)(2,1)}, f32[1,8,1024]{2,1,0:T(8,128)}) custom-call(bf16[1024,384]{1,0:T(8,128)(2,1)} %q_ref.7, bf16[1024,384]{1,0:T(8,128)(2,1)} %k_ref.7, bf16[1024,384]{1,0:T(8,128)(2,1)} %v_ref.7), custom_call_target="tpu_custom_call" | custom-call | flops 536870912 | bytes 1048576 | tf_op jit(solution)/shard_map/near/pallas_call | solution.py:159
  82.3 0.0 all-to-all-done.2.refs_6_
  82.3 0.0 copy-start
  82.3 0.7 copy-done
  83.0 3.4 %merge.1 = bf16[1024,384]{1,0:T(8,128)(2,1)} custom-call(bf16[128,1024]{1,0:T(8,128)(2,1)} %get-tuple-element.13.refs_0_, bf16[128,1024]{1,0:T(8,128)(2,1)} %get-tuple-element.14.refs_1_, bf16[128,1024]{1,0:T(8,128)(2,1)} %get-tuple-element.15.refs_2_, f32[1,8,1024]{2,1,0:T(8,128)} %get-tuple-element.16.refs_3_, f32[1,8,1024]{2,1,0:T(8,128)} %get-tuple-element.17.refs_4_, ...), custom_call_target="tpu_custom_call" | custom-call | tf_op jit(solution)/shard_map/merge/pallas_call | solution.py:350
Async XLA Ops:
  26.9 26.9 %all-to-all-start.1 = ((bf16[16,48,128]{2,1,0:T(8,128)(2,1)}), bf16[16,48,128]{2,1,0:T(8,128)(2,1)S(1)}, u32[]{:S(2)}, u32[]{:S(2)}) async-start(bf16[16,48,128]{2,1,0:T(8,128)(2,1)} %get-tuple-element.20), calls=%async_computation.1 | async-start | bytes 393216 | tf_op jit(solution)/shard_map/all_to_all | solution.py:362
  53.8 0.7 copy-start.1
  57.9 24.4 %all-to-all-start.2 = ((bf16[8,112,128]{2,1,0:T(8,128)(2,1)}), bf16[8,112,128]{2,1,0:T(8,128)(2,1)S(1)}, u32[]{:S(2)}, u32[]{:S(2)}) async-start(bf16[8,112,128]{2,1,0:T(8,128)(2,1)} %far.1), calls=%async_computation.2 | async-start | bytes 458752 | tf_op jit(solution)/shard_map/all_to_all | solution.py:370
  82.3 0.7 copy-start

commit v2 on v1

--- a/solution.py
+++ b/solution.py
@@ -30,6 +30,19 @@
 BACK = BACK_MID + (PAIRS + 1) * FAR
 
 
+def held_call(kernel, out_shapes, *operands, room=8, **options):
+    outs = tuple(pltpu.VMEM(shape, dtype) for shape, dtype in out_shapes)
+    space = pl.BlockSpec(memory_space=pltpu.VMEM)
+    return pl.pallas_call(
+        kernel,
+        out_shape=outs,
+        in_specs=[space] * len(operands),
+        out_specs=(space,) * len(outs),
+        compiler_params=pltpu.CompilerParams(vmem_limit_bytes=room * 2**20),
+        **options,
+    )(*[pltpu.with_memory_space_constraint(x, pltpu.VMEM) for x in operands])
+
+
 def dot(a, b, dims):
     return lax.dot_general(a, b, dims, preferred_element_type=F32)
 
@@ -46,16 +59,29 @@
     return high, middle, low
 
 
-def pack_kernel(q_ref, k_ref, v_ref, mid_ref, far_ref, q_wide, k_wide, v_wide):
+def pack_kernel(*refs):
+    sources, refs = refs[:3], refs[3:]
+    mid_ref, far_ref = refs[:2]
+    copies, (q_wide, k_wide, v_wide, sems) = refs[2:-4], refs[-4:]
+    moves = []
+    for pair in range(PAIRS):
+        for place, source in enumerate(sources):
+            slot = 3 * pair + place
+            move = pltpu.make_async_copy(
+                source.at[:, pair * LANES : (pair + 1) * LANES], copies[slot], sems.at[slot]
+            )
+            move.start()
+            moves.append(move)
     far_q, far_k, far_v = [], [], []
     low_mid = lane_low((MID, LANES))
     low_half = lane_low((MID // 2, LANES))
     low_far = lane_low((FAR, LANES))
+    for spare in range(HEADS, SEG):
+        mid_ref[spare, 0 : MID + MID // 2, :] = jnp.zeros((MID + MID // 2, LANES), BF16)
     for pair in range(PAIRS):
-        cols = slice(pair * LANES, (pair + 1) * LANES)
-        q_wide[...] = q_ref[:, cols].astype(F32)
-        k_wide[...] = k_ref[:, cols].astype(F32)
-        v_wide[...] = v_ref[:, cols].astype(F32)
+        for place, wide in enumerate((q_wide, k_wide, v_wide)):
+            moves[3 * pair + place].wait()
+            wide[...] = copies[3 * pair + place][...].astype(F32)
         for side in range(2):
             head = 2 * pair + side
             q_rows = q_wide[pl.ds(head, MID, stride=SEG), :]
@@ -77,26 +103,26 @@
             first = wide[pl.ds(2 * pair, FAR, stride=FAR_PERIOD), :]
             second = wide[pl.ds(2 * pair + 1, FAR, stride=FAR_PERIOD), :]
             out.append(jnp.where(low_far, first, second))
-    for spare in range(HEADS, SEG):
-        mid_ref[spare, 0 : MID + MID // 2, :] = jnp.zeros((MID + MID // 2, LANES), BF16)
     tail = jnp.concatenate(far_q + [jnp.zeros((FAR, LANES), F32)], axis=0).astype(BF16)
     for target in range(SEG):
         mid_ref[target, MID + MID // 2 : SEND_MID, :] = tail
-    both = jnp.concatenate(far_k + far_v, axis=0).astype(BF16)
-    for target in range(SLIDE_GRP):
-        far_ref[target] = both
+    far_ref[0] = jnp.concatenate(far_k + far_v, axis=0).astype(BF16)
 
 
 def pack(queries, keys, values):
+    shapes = [((SEG, SEND_MID, LANES), BF16), ((1, 2 * PAIRS * FAR, LANES), BF16)]
+    shapes += [((ROWS, LANES), BF16)] * (3 * PAIRS)
+    space = pl.BlockSpec(memory_space=pltpu.VMEM)
     return pl.pallas_call(
         pack_kernel,
-        out_shape=(
-            jax.ShapeDtypeStruct((SEG, SEND_MID, LANES), BF16),
-            jax.ShapeDtypeStruct((SLIDE_GRP, 2 * PAIRS * FAR, LANES), BF16),
-        ),
-        scratch_shapes=[pltpu.VMEM((ROWS, LANES), F32)] * 3,
+        out_shape=tuple(pltpu.VMEM(shape, dtype) for shape, dtype in shapes),
+        in_specs=[pl.BlockSpec(memory_space=pl.ANY)] * 3,
+        out_specs=(space,) * len(shapes),
+        scratch_shapes=[pltpu.VMEM((ROWS, LANES), F32)] * 3
+        + [pltpu.SemaphoreType.DMA((3 * PAIRS,))],
+        compiler_params=pltpu.CompilerParams(vmem_limit_bytes=8 * 2**20),
         name="pack",
-    )(queries, keys, values)
+    )(*[pltpu.with_memory_space_constraint(x, pltpu.HBM) for x in (queries, keys, values)])
 
 
 def scores_of(key_rows, query_rows):
@@ -154,27 +180,21 @@
     )
 
 
-def near(queries, keys, values, first, count):
-    spec = pl.BlockSpec((ROWS, LANES), lambda i: (0, i + first))
-    return pl.pallas_call(
+def near(queries, keys, values):
+    return held_call(
         near_kernel,
-        grid=(count,),
-        in_specs=[spec] * 3,
-        out_specs=(
-            pl.BlockSpec((LANES, ROWS), lambda i: (i, 0)),
-            pl.BlockSpec((1, 8, ROWS), lambda i: (i, 0, 0)),
+        [((LANES, ROWS), BF16), ((1, 8, ROWS), F32)],
+        queries,
+        keys,
+        values,
+        cost_estimate=pl.CostEstimate(
+            flops=2 * 4 * ROWS * ROWS * HEAD_WIDTH,
+            bytes_accessed=4 * ROWS * LANES * 2,
+            transcendentals=2 * ROWS * ROWS,
         ),
-        out_shape=(
-            jax.ShapeDtypeStruct((count * LANES, ROWS), BF16),
-            jax.ShapeDtypeStruct((count, 8, ROWS), F32),
-        ),
-        cost_estimate=pl.CostEstimate(
-            flops=count * 2 * 4 * ROWS * ROWS * HEAD_WIDTH,
-            bytes_accessed=count * 4 * ROWS * LANES * 2,
-            transcendentals=count * 2 * ROWS * ROWS,
-        ),
+        room=16,
         name="near",
-    )(queries, keys, values)
+    )
 
 
 def mid_kernel(r_ref, s_ref):
@@ -206,21 +226,24 @@
 
 
 def mid(received):
-    return pl.pallas_call(
+    return held_call(
         mid_kernel,
-        out_shape=jax.ShapeDtypeStruct((SEG, BACK_MID, MID), BF16),
+        [((SEG, BACK_MID, MID), BF16)],
+        received,
         cost_estimate=pl.CostEstimate(
             flops=4 * ROWS * ROWS * HEAD_WIDTH,
             bytes_accessed=ROWS * LANES * 4,
             transcendentals=ROWS * ROWS,
         ),
+        room=16,
         name="mid",
-    )(received)
-
-
-def far_kernel(r_ref, f_ref, m_ref, s_ref):
+    )[0]
+
+
+def far_kernel(r_ref, *refs):
+    m_ref, s_ref = refs[-2:]
     queries = r_ref[:, MID + MID // 2 : SEND_MID, :].astype(F32) * SCALE
-    others = f_ref[...].astype(F32)
+    others = jnp.concatenate([ref[...] for ref in refs[:-2]], axis=0).astype(F32)
     count = SEG * FAR
     low = lane_low((count, LANES))
     lane = lax.broadcasted_iota(jnp.int32, (count, LANES), 1)
@@ -255,17 +278,15 @@
 
 
 def far(received, others, mid_part):
-    return pl.pallas_call(
-        far_kernel,
-        out_shape=jax.ShapeDtypeStruct((SEG, BACK, LANES), BF16),
-        name="far",
-    )(received, others, mid_part)
+    return held_call(
+        far_kernel, [((SEG, BACK, LANES), BF16)], received, *others, mid_part, name="far"
+    )[0]
 
 
 def merge_kernel(*refs):
-    n = (len(refs) - 2) // 2
-    near_refs, lse_refs = refs[:n], refs[n : 2 * n]
-    back_ref, out_ref = refs[2 * n :]
+    near_refs, lse_refs = refs[:PAIRS], refs[PAIRS : 2 * PAIRS]
+    back_ref, out_ref, stage_ref, sems = refs[2 * PAIRS :]
+    moves = []
     width = HEADS * HEAD_WIDTH
     parts = back_ref[:, BACK_MID:, :].astype(F32)
     count = SEG * FAR
@@ -340,33 +361,54 @@
                 ].astype(F32)
                 sides.append(rest * own + share * spread[:HEAD_WIDTH])
             whole = start // 2 + pair
-            out_ref[:, whole * LANES : (whole + 1) * LANES] = (
-                jnp.concatenate(sides, axis=0).astype(BF16).T
+            stage_ref[whole] = jnp.concatenate(sides, axis=0).astype(BF16).T
+            move = pltpu.make_async_copy(
+                stage_ref.at[whole],
+                out_ref.at[:, whole * LANES : (whole + 1) * LANES],
+                sems.at[whole],
             )
+            move.start()
+            moves.append(move)
         start += 2 * (ref.shape[0] // LANES)
+    for move in moves:
+        move.wait()
 
 
 def merge(near_outs, near_lses, back):
+    operands = (*near_outs, *near_lses, back)
     return pl.pallas_call(
         merge_kernel,
         out_shape=jax.ShapeDtypeStruct((ROWS, HEADS * HEAD_WIDTH), BF16),
+        in_specs=[pl.BlockSpec(memory_space=pltpu.VMEM)] * len(operands),
+        out_specs=pl.BlockSpec(memory_space=pl.ANY),
+        scratch_shapes=[
+            pltpu.VMEM((PAIRS, ROWS, LANES), BF16),
+            pltpu.SemaphoreType.DMA((PAIRS,)),
+        ],
+        compiler_params=pltpu.CompilerParams(vmem_limit_bytes=16 * 2**20),
         name="merge",
-    )(*near_outs, *near_lses, back)
+    )(*[pltpu.with_memory_space_constraint(x, pltpu.VMEM) for x in operands])
+
+
+def fan_out(held, masks):
+    size = lax.axis_size("grp")
+    got = []
+    for mask in masks:
+        got.append(lax.ppermute(held, "grp", [(i, i ^ mask) for i in range(size)]))
+    return got
 
 
 def body(queries, keys, values):
-    groups = lax.axis_size("grp") // SLIDE_GRP
-    slides = [[s * SLIDE_GRP + i for i in range(SLIDE_GRP)] for s in range(groups)]
-    mid_send, far_send = pack(queries, keys, values)
+    mid_send, held, *pieces = pack(queries, keys, values)
     mid_got = lax.all_to_all(mid_send, "seg", 0, 0, tiled=True)
-    far_got = lax.all_to_all(
-        far_send, "grp", 0, 0, tiled=True, axis_index_groups=slides
-    )
+    for mask in (8, 4):
+        held = jnp.concatenate([held] + fan_out(held, (mask,)), axis=0)
+    inner = fan_out(held, (1, 3, 2))
     nears = []
     for pair in range(3):
-        nears.append(near(queries, keys, values, pair, 1))
+        nears.append(near(*pieces[3 * pair : 3 * pair + 3]))
     mid_part = mid(mid_got)
-    part = far(mid_got, far_got, mid_part)
+    part = far(mid_got, (held, *inner), mid_part)
     back = lax.all_to_all(part, "seg", 0, 0, tiled=True)
     return merge([n[0] for n in nears], [n[1] for n in nears], back)
 

time: 86.9 us -> 75.1 us (0.86)
  blocking collectives: 23.9 us -> 0 us
  starting transfers between devices: 20.3 us -> 42 us
  Pallas kernels: 29.7 us -> 19.6 us
  waiting for transfers between devices: 11.1 us -> 12.6 us
  local copies, waits for them, and re-layouts: 1.35 us -> 0.02 us
    all_to_all x1 -> x0, blocking collectives: 23.9 us -> none  [body(): mid_got = lax.all_to_all(mid_send, 'seg', 0, 0, tiled=True)]
    ppermute x0 -> x5, starting transfers between devices: none -> 23.2 us  [fan_out(): got.append(lax.ppermute(held, 'grp', [(i, i ^ mask) for i in range(size)]))]
    ppermute x0 -> x5, waiting for transfers between devices: none -> 12.6 us  [fan_out(): got.append(lax.ppermute(held, 'grp', [(i, i ^ mask) for i in range(size)]))]
    all_to_all x1, waiting for transfers between devices: 11.1 us -> 0.01 us  [body(): mid_got = lax.all_to_all(mid_send, 'seg', 0, 0, tiled=True)]
    pallas_call x6, Pallas kernels: 26.4 us -> 17.6 us  [the longest x5 15 us: held_call(): pl.pallas_call(kernel, out_shape=outs, in_specs=[space] * len(operands),...]
    all_to_all x1, starting transfers between devices: 12.2 us -> 10.2 us  [body(): mid_got = lax.all_to_all(mid_send, 'seg', 0, 0, tiled=True)]
    pallas_call x1, Pallas kernels: 3.38 us -> 2.02 us  [merge(): pl.pallas_call(merge_kernel, out_shape=jax.ShapeDtypeStruct((ROWS, HEADS...]
    unnamed x4 -> x2, local copies, waits for them, and re-layouts: 1.35 us -> 0.01 us
  transfers between devices with their start and end apart: 2 -> 7, of which waited for: 1 -> 3; matrix products, arithmetic and copies ran while one was open for 0% -> 0% of each run, Pallas kernels for 23% -> 17%
where the time goes in v2:
time: 75.1 us; the launch traced here: 74.6 us
  starting transfers between devices  42 us (56%)
  Pallas kernels  19.6 us (26%)
  waiting for transfers between devices  12.6 us (17%)
    ppermute x5, starting transfers between devices, fan_out(): got.append(lax.ppermute(held, 'grp', [(i, i ^ mask) for i in range(size)]))  23.2 us
    pallas_call x5, Pallas kernels, held_call(): pl.pallas_call(kernel, out_shape=outs, in_specs=[space] * len(operands),...  15 us
    ppermute x5, waiting for transfers between devices, fan_out(): got.append(lax.ppermute(held, 'grp', [(i, i ^ mask) for i in range(size)]))  12.6 us
    all_to_all x1, starting transfers between devices, body(): mid_got = lax.all_to_all(mid_send, 'seg', 0, 0, tiled=True)  10.2 us
    all_to_all x1, starting transfers between devices, body(): back = lax.all_to_all(part, 'seg', 0, 0, tiled=True)  8.57 us
    pallas_call x1, Pallas kernels, pack(): pl.pallas_call(pack_kernel, out_shape=tuple((pltpu.VMEM(shape, dtype) for...  2.58 us
    pallas_call x1, Pallas kernels, merge(): pl.pallas_call(merge_kernel, out_shape=jax.ShapeDtypeStruct((ROWS, HEADS...  2.02 us
  transfers between devices with their start and end apart: 7, of which 3 were waited for; matrix products, arithmetic and copies ran while one was open for 0% of the time, Pallas kernels for 17%

profile of v2, /device:TPU:1, one launch (start us, length us, event | category | flops | bytes accessed | tf_op | source)
XLA Modules:
  0.0 74.6 jit_solution(1766201644791565803)
XLA Ops:
  0.0 2.6 %pack.1 = (bf16[8,224,128]{2,1,0:T(8,128)(2,1)}, bf16[1,48,128]{2,1,0:T(8,128)(2,1)S(1)}, bf16[1024,128]{1,0:T(8,128)(2,1)S(1)}, bf16[1024,128]{1,0:T(8,128)(2,1...) custom-call(bf16[1024,384]{1,0:T(8,128)(2,1)} %refs_0_.1, ...), custom_call_target="tpu_custom_call" | custom-call | tf_op jit(solution)/shard_map/pack/pallas_call | solution.py:116
  2.6 10.2 %all-to-all-start = ((bf16[8,224,128]{2,1,0:T(8,128)(2,1)}), bf16[8,224,128]{2,1,0:T(8,128)(2,1)S(1)}, u32[]{:S(2)}, u32[]{:S(2)}) async-start(bf16[8,224,128]{2,1,0:T(8,128)(2,1)} %get-tuple-element.37), calls=%async_computation | async-start | bytes 917504 | tf_op jit(solution)/shard_map/all_to_all | solution.py:403
  12.8 10.1 %collective-permute-start = (bf16[1,48,128]{2,1,0:T(8,128)(2,1)S(1)}, bf16[1,48,128]{2,1,0:T(8,128)(2,1)S(1)}, u32[]{:S(2)}, u32[]{:S(2)}) collective-permute-start(bf16[1,48,128]{2,1,0:T(8,128)(2,1)S(1)} %get-tuple-element.38), channel_id=1, source_target_pairs={{0,64},{8,72},{16,80},{24,88},{32,96},{40,104},{48,112},{56,120},{... | collective-permute-start | bytes 36872 | tf_op jit(solution)/shard_map/ppermute | solution.py:397
  22.9 6.7 %collective-permute-done = bf16[1,48,128]{2,1,0:T(8,128)(2,1)S(1)} collective-permute-done((bf16[1,48,128]{2,1,0:T(8,128)(2,1)S(1)}, bf16[1,48,128]{2,1,0:T(8,128)(2,1)S(1)}, u32[]{:S(2)}, u32[]{:S(2)}) %collective-permute-start) | collective-permute-done | bytes 12320 | tf_op jit(solution)/shard_map/ppermute | solution.py:397
  29.7 4.0 %collective-permute-start.1 = (bf16[2,48,128]{2,1,0:T(8,128)(2,1)S(1)}, bf16[2,48,128]{2,1,0:T(8,128)(2,1)S(1)}, u32[]{:S(2)}, u32[]{:S(2)}) collective-permute-start(bf16[2,48,128]{2,1,0:T(8,128)(2,1)S(1)} %pad_maximum_fusion), channel_id=1, source_target_pairs={{0,32},{8,40},{16,48},{24,56},{32,0},{40,8},{48,16},{56,24},{64,96... | collective-permute-start | bytes 73736 | tf_op jit(solution)/shard_map/ppermute | solution.py:397
  33.7 5.0 %collective-permute-done.1 = bf16[2,48,128]{2,1,0:T(8,128)(2,1)S(1)} collective-permute-done((bf16[2,48,128]{2,1,0:T(8,128)(2,1)S(1)}, bf16[2,48,128]{2,1,0:T(8,128)(2,1)S(1)}, u32[]{:S(2)}, u32[]{:S(2)}) %collective-permute-start.1) | collective-permute-done | bytes 24608 | tf_op jit(solution)/shard_map/ppermute | solution.py:397
  38.7 4.5 %collective-permute-start.4 = (bf16[4,48,128]{2,1,0:T(8,128)(2,1)S(1)}, bf16[4,48,128]{2,1,0:T(8,128)(2,1)S(1)}, u32[]{:S(2)}, u32[]{:S(2)}) collective-permute-start(bf16[4,48,128]{2,1,0:T(8,128)(2,1)S(1)} %constant_dynamic-update-slice_fusion.refs_0_), channel_id=1, source_target_pairs={{0,16},{8,24},{16,0},{24,8},{32,48},{40,56},{48,32},{56,40},{64,80... | collective-permute-start | bytes 147464 | tf_op jit(solution)/shard_map/ppermute | solution.py:397
  43.2 2.7 %collective-permute-start.3 = (bf16[4,48,128]{2,1,0:T(8,128)(2,1)S(1)}, bf16[4,48,128]{2,1,0:T(8,128)(2,1)S(1)}, u32[]{:S(2)}, u32[]{:S(2)}) collective-permute-start(bf16[4,48,128]{2,1,0:T(8,128)(2,1)S(1)} %constant_dynamic-update-slice_fusion.refs_0_), channel_id=1, source_target_pairs={{0,24},{8,16},{16,8},{24,0},{32,56},{40,48},{48,40},{56,32},{64,88... | collective-permute-start | bytes 147464 | tf_op jit(solution)/shard_map/ppermute | solution.py:397
  45.9 1.9 %collective-permute-start.2 = (bf16[4,48,128]{2,1,0:T(8,128)(2,1)S(1)}, bf16[4,48,128]{2,1,0:T(8,128)(2,1)S(1)}, u32[]{:S(2)}, u32[]{:S(2)}) collective-permute-start(bf16[4,48,128]{2,1,0:T(8,128)(2,1)S(1)} %constant_dynamic-update-slice_fusion.refs_0_), channel_id=1, source_target_pairs={{0,8},{8,0},{16,24},{24,16},{32,40},{40,32},{48,56},{56,48},{64,72... | collective-permute-start | bytes 147464 | tf_op jit(solution)/shard_map/ppermute | solution.py:397
  47.8 0.0 all-to-all-done.r_ref
  47.9 2.0 %mid.1.refs_4_ = bf16[8,80,128]{2,1,0:T(8,128)(2,1)S(1)} custom-call(bf16[8,224,128]{2,1,0:T(8,128)(2,1)S(1)} %all-to-all-done.r_ref), custom_call_target="tpu_custom_call" | custom-call | flops 268435456 | bytes 524288 | tf_op jit(solution)/shard_map/mid/pallas_call | solution.py:36
  49.8 0.0 collective-permute-done.4.refs_3_
  49.8 0.0 collective-permute-done.3.refs_2_
  49.8 0.9 %collective-permute-done.2.refs_1_ = bf16[4,48,128]{2,1,0:T(8,128)(2,1)S(1)} collective-permute-done((bf16[4,48,128]{2,1,0:T(8,128)(2,1)S(1)}, bf16[4,48,128]{2,1,0:T(8,128)(2,1)S(1)}, u32[]{:S(2)}, u32[]{:S(2)}) %collective-permute-start.2) | collective-permute-done | bytes 49184 | tf_op jit(solution)/shard_map/ppermute | solution.py:397
  50.7 2.2 %far.1 = bf16[8,112,128]{2,1,0:T(8,128)(2,1)} custom-call(bf16[8,224,128]{2,1,0:T(8,128)(2,1)S(1)} %all-to-all-done.r_ref, bf16[4,48,128]{2,1,0:T(8,128)(2,1)S(1)} %constant_dynamic-update-slice_fusion.refs_0_, bf16[4,48,128]{2,1,0:T(8,128)(2,1)S(1)} %collective-permute-done.2.refs_1_, bf16[4,48,128]{2,1,0:T(8,128)(2,1)S(1)} %collective-permute-done.3.refs_2_, ...), custom_call_target="tpu_custom_call" | custom-call | tf_op jit(solution)/shard_map/far/pallas_call | solution.py:36
  53.0 8.6 %all-to-all-start.1 = ((bf16[8,112,128]{2,1,0:T(8,128)(2,1)}), bf16[8,112,128]{2,1,0:T(8,128)(2,1)S(1)}, u32[]{:S(2)}, u32[]{:S(2)}) async-start(bf16[8,112,128]{2,1,0:T(8,128)(2,1)} %far.1), calls=%async_computation.1 | async-start | bytes 458752 | tf_op jit(solution)/shard_map/all_to_all | solution.py:412
  61.5 3.6 %near.3 = (bf16[128,1024]{1,0:T(8,128)(2,1)S(1)}, f32[1,8,1024]{2,1,0:T(8,128)S(1)}) custom-call(bf16[1024,128]{1,0:T(8,128)(2,1)S(1)} %get-tuple-element.22.q_ref, bf16[1024,128]{1,0:T(8,128)(2,1)S(1)} %get-tuple-element.23.k_ref, bf16[1024,128]{1,0:T(8,128)(2,1)S(1)} %get-tuple-element.24.v_ref), custom_call_target="tpu_custom_call" | custom-call | flops 536870912 | bytes 1048576 | tf_op jit(solution)/shard_map/near/pallas_call | solution.py:36
  65.2 3.6 %near.4 = (bf16[128,1024]{1,0:T(8,128)(2,1)S(1)}, f32[1,8,1024]{2,1,0:T(8,128)S(1)}) custom-call(bf16[1024,128]{1,0:T(8,128)(2,1)S(1)} %get-tuple-element.26.q_ref, bf16[1024,128]{1,0:T(8,128)(2,1)S(1)} %get-tuple-element.27.k_ref, bf16[1024,128]{1,0:T(8,128)(2,1)S(1)} %get-tuple-element.28.v_ref), custom_call_target="tpu_custom_call" | custom-call | flops 536870912 | bytes 1048576 | tf_op jit(solution)/shard_map/near/pallas_call | solution.py:36
  68.8 3.6 %near.5 = (bf16[128,1024]{1,0:T(8,128)(2,1)S(1)}, f32[1,8,1024]{2,1,0:T(8,128)S(1)}) custom-call(bf16[1024,128]{1,0:T(8,128)(2,1)S(1)} %get-tuple-element.30.q_ref, bf16[1024,128]{1,0:T(8,128)(2,1)S(1)} %get-tuple-element.31.k_ref, bf16[1024,128]{1,0:T(8,128)(2,1)S(1)} %get-tuple-element.32.v_ref), custom_call_target="tpu_custom_call" | custom-call | flops 536870912 | bytes 1048576 | tf_op jit(solution)/shard_map/near/pallas_call | solution.py:36
  72.4 0.0 all-to-all-done.1.refs_6_
  72.4 2.0 %merge.1 = bf16[1024,384]{1,0:T(8,128)(2,1)} custom-call(bf16[128,1024]{1,0:T(8,128)(2,1)S(1)} %get-tuple-element.25.refs_0_, bf16[128,1024]{1,0:T(8,128)(2,1)S(1)} %get-tuple-element.29.refs_1_, bf16[128,1024]{1,0:T(8,128)(2,1)S(1)} %get-tuple-element.33.refs_2_, f32[1,8,1024]{2,1,0:T(8,128)S(1)} %get-tuple-element.34.refs_3_, ...), custom_call_target="tpu_custom_call" | custom-call | tf_op jit(solution)/shard_map/merge/pallas_call | solution.py:379
  (4 shorter events, 0.0 us)
Async XLA Ops:
  2.6 45.3 %all-to-all-start = ((bf16[8,224,128]{2,1,0:T(8,128)(2,1)}), bf16[8,224,128]{2,1,0:T(8,128)(2,1)S(1)}, u32[]{:S(2)}, u32[]{:S(2)}) async-start(bf16[8,224,128]{2,1,0:T(8,128)(2,1)} %get-tuple-element.37), calls=%async_computation | async-start | bytes 917504 | tf_op jit(solution)/shard_map/all_to_all | solution.py:403
  12.8 16.8 %collective-permute-start = (bf16[1,48,128]{2,1,0:T(8,128)(2,1)S(1)}, bf16[1,48,128]{2,1,0:T(8,128)(2,1)S(1)}, u32[]{:S(2)}, u32[]{:S(2)}) collective-permute-start(bf16[1,48,128]{2,1,0:T(8,128)(2,1)S(1)} %get-tuple-element.38), channel_id=1, source_target_pairs={{0,64},{8,72},{16,80},{24,88},{32,96},{40,104},{48,112},{56,120},{... | collective-permute-start | bytes 36872 | tf_op jit(solution)/shard_map/ppermute | solution.py:397
  29.7 9.0 %collective-permute-start.1 = (bf16[2,48,128]{2,1,0:T(8,128)(2,1)S(1)}, bf16[2,48,128]{2,1,0:T(8,128)(2,1)S(1)}, u32[]{:S(2)}, u32[]{:S(2)}) collective-permute-start(bf16[2,48,128]{2,1,0:T(8,128)(2,1)S(1)} %pad_maximum_fusion), channel_id=1, source_target_pairs={{0,32},{8,40},{16,48},{24,56},{32,0},{40,8},{48,16},{56,24},{64,96... | collective-permute-start | bytes 73736 | tf_op jit(solution)/shard_map/ppermute | solution.py:397
  38.7 11.2 %collective-permute-start.4 = (bf16[4,48,128]{2,1,0:T(8,128)(2,1)S(1)}, bf16[4,48,128]{2,1,0:T(8,128)(2,1)S(1)}, u32[]{:S(2)}, u32[]{:S(2)}) collective-permute-start(bf16[4,48,128]{2,1,0:T(8,128)(2,1)S(1)} %constant_dynamic-update-slice_fusion.refs_0_), channel_id=1, source_target_pairs={{0,16},{8,24},{16,0},{24,8},{32,48},{40,56},{48,32},{56,40},{64,80... | collective-permute-start | bytes 147464 | tf_op jit(solution)/shard_map/ppermute | solution.py:397
  43.2 6.6 %collective-permute-start.3 = (bf16[4,48,128]{2,1,0:T(8,128)(2,1)S(1)}, bf16[4,48,128]{2,1,0:T(8,128)(2,1)S(1)}, u32[]{:S(2)}, u32[]{:S(2)}) collective-permute-start(bf16[4,48,128]{2,1,0:T(8,128)(2,1)S(1)} %constant_dynamic-update-slice_fusion.refs_0_), channel_id=1, source_target_pairs={{0,24},{8,16},{16,8},{24,0},{32,56},{40,48},{48,40},{56,32},{64,88... | collective-permute-start | bytes 147464 | tf_op jit(solution)/shard_map/ppermute | solution.py:397
  45.9 4.8 %collective-permute-start.2 = (bf16[4,48,128]{2,1,0:T(8,128)(2,1)S(1)}, bf16[4,48,128]{2,1,0:T(8,128)(2,1)S(1)}, u32[]{:S(2)}, u32[]{:S(2)}) collective-permute-start(bf16[4,48,128]{2,1,0:T(8,128)(2,1)S(1)} %constant_dynamic-update-slice_fusion.refs_0_), channel_id=1, source_target_pairs={{0,8},{8,0},{16,24},{24,16},{32,40},{40,32},{48,56},{56,48},{64,72... | collective-permute-start | bytes 147464 | tf_op jit(solution)/shard_map/ppermute | solution.py:397
  53.0 19.5 %all-to-all-start.1 = ((bf16[8,112,128]{2,1,0:T(8,128)(2,1)}), bf16[8,112,128]{2,1,0:T(8,128)(2,1)S(1)}, u32[]{:S(2)}, u32[]{:S(2)}) async-start(bf16[8,112,128]{2,1,0:T(8,128)(2,1)} %far.1), calls=%async_computation.1 | async-start | bytes 458752 | tf_op jit(solution)/shard_map/all_to_all | solution.py:412

commit v3 on v2

--- a/solution.py
+++ b/solution.py
@@ -16,6 +16,7 @@
 FAR_PERIOD = SLIDE_GRP * SEG
 FAR = ROWS // FAR_PERIOD
 CHUNK = 256
+BLOCK = 256
 SCALE = HEAD_WIDTH ** (-0.5)
 
 
@@ -25,8 +26,8 @@
 F32 = jnp.float32
 BF16 = jnp.bfloat16
 
-SEND_MID = 224
-BACK_MID = 80
+SEND_MID = 216
+BACK_MID = 72
 BACK = BACK_MID + (PAIRS + 1) * FAR
 
 
@@ -59,10 +60,46 @@
     return high, middle, low
 
 
+def pack_far_kernel(k_ref, v_ref, far_ref, taken, wide, sems):
+    moves = []
+    for place, source in enumerate((k_ref, v_ref)):
+        move = pltpu.make_async_copy(source.at[:, 0:SEG, :], taken.at[place], sems.at[place])
+        move.start()
+        moves.append(move)
+    low = lane_low((FAR, LANES))
+    rows = []
+    for place, move in enumerate(moves):
+        move.wait()
+        for pair in range(PAIRS):
+            lanes = slice(pair * LANES, (pair + 1) * LANES)
+            wide[...] = taken[place, :, :, lanes].astype(F32).reshape(FAR * SEG, LANES)
+            first = wide[pl.ds(2 * pair, FAR, stride=SEG), :]
+            second = wide[pl.ds(2 * pair + 1, FAR, stride=SEG), :]
+            rows.append(jnp.where(low, first, second))
+    far_ref[0] = jnp.concatenate(rows, axis=0).astype(BF16)
+
+
+def pack_far(keys, values):
+    width = HEADS * HEAD_WIDTH
+    operands = [x.reshape(FAR, FAR_PERIOD, width) for x in (keys, values)]
+    return pl.pallas_call(
+        pack_far_kernel,
+        out_shape=pltpu.VMEM((1, 2 * PAIRS * FAR, LANES), BF16),
+        in_specs=[pl.BlockSpec(memory_space=pl.ANY)] * 2,
+        out_specs=pl.BlockSpec(memory_space=pltpu.VMEM),
+        scratch_shapes=[
+            pltpu.VMEM((2, FAR, SEG, width), BF16),
+            pltpu.VMEM((FAR * SEG, LANES), F32),
+            pltpu.SemaphoreType.DMA((2,)),
+        ],
+        compiler_params=pltpu.CompilerParams(vmem_limit_bytes=4 * 2**20),
+        name="pack_far",
+    )(*[pltpu.with_memory_space_constraint(x, pltpu.HBM) for x in operands])
+
+
 def pack_kernel(*refs):
     sources, refs = refs[:3], refs[3:]
-    mid_ref, far_ref = refs[:2]
-    copies, (q_wide, k_wide, v_wide, sems) = refs[2:-4], refs[-4:]
+    mid_ref, copies, (q_wide, k_wide, v_wide, sems) = refs[0], refs[1:-4], refs[-4:]
     moves = []
     for pair in range(PAIRS):
         for place, source in enumerate(sources):
@@ -72,7 +109,7 @@
             )
             move.start()
             moves.append(move)
-    far_q, far_k, far_v = [], [], []
+    far_q = []
     low_mid = lane_low((MID, LANES))
     low_half = lane_low((MID // 2, LANES))
     low_far = lane_low((FAR, LANES))
@@ -99,19 +136,16 @@
                 )
             mid_ref[head, 0:MID, :] = key_value.astype(BF16)
             mid_ref[head, MID : MID + MID // 2, :] = query.astype(BF16)
-        for wide, out in ((q_wide, far_q), (k_wide, far_k), (v_wide, far_v)):
-            first = wide[pl.ds(2 * pair, FAR, stride=FAR_PERIOD), :]
-            second = wide[pl.ds(2 * pair + 1, FAR, stride=FAR_PERIOD), :]
-            out.append(jnp.where(low_far, first, second))
-    tail = jnp.concatenate(far_q + [jnp.zeros((FAR, LANES), F32)], axis=0).astype(BF16)
+        first = q_wide[pl.ds(2 * pair, FAR, stride=FAR_PERIOD), :]
+        second = q_wide[pl.ds(2 * pair + 1, FAR, stride=FAR_PERIOD), :]
+        far_q.append(jnp.where(low_far, first, second))
+    tail = jnp.concatenate(far_q, axis=0).astype(BF16)
     for target in range(SEG):
         mid_ref[target, MID + MID // 2 : SEND_MID, :] = tail
-    far_ref[0] = jnp.concatenate(far_k + far_v, axis=0).astype(BF16)
 
 
 def pack(queries, keys, values):
-    shapes = [((SEG, SEND_MID, LANES), BF16), ((1, 2 * PAIRS * FAR, LANES), BF16)]
-    shapes += [((ROWS, LANES), BF16)] * (3 * PAIRS)
+    shapes = [((SEG, SEND_MID, LANES), BF16)] + [((ROWS, LANES), BF16)] * (3 * PAIRS)
     space = pl.BlockSpec(memory_space=pltpu.VMEM)
     return pl.pallas_call(
         pack_kernel,
@@ -125,25 +159,30 @@
     )(*[pltpu.with_memory_space_constraint(x, pltpu.HBM) for x in (queries, keys, values)])
 
 
-def scores_of(key_rows, query_rows):
-    return dot(key_rows, query_rows, NT)
-
-
-def finish(scores, value_columns):
-    highest = jnp.max(scores, axis=0, keepdims=True)
-    raised = jnp.exp(scores - highest).astype(BF16)
-    mixed = dot(value_columns, raised, NN)
-    totals = mixed[HEAD_WIDTH : HEAD_WIDTH + 1]
-    return mixed[:HEAD_WIDTH] / totals, highest + jnp.log(totals)
-
-
 def chunks_of(key_rows, query_parts, value_parts, put):
     count = len(query_parts)
-    pending = scores_of(key_rows, query_parts[0]())
+    blocks = [slice(at, at + BLOCK) for at in range(0, ROWS, BLOCK)]
+
+    def top_of(tiles):
+        best = tiles[0]
+        for tile in tiles[1:]:
+            best = jnp.maximum(best, tile)
+        return jnp.max(best, axis=0, keepdims=True)
+
+    query = query_parts[0]()
+    pending = [dot(key_rows[block], query, NT) for block in blocks]
     for step in range(count):
-        following = scores_of(key_rows, query_parts[step + 1]()) if step + 1 < count else None
-        mixed, lse = finish(pending, value_parts[step])
-        put(step, mixed, lse)
+        highest = top_of(pending)
+        query = query_parts[step + 1]() if step + 1 < count else None
+        following, mixed = [], None
+        raised = []
+        for block, tile in zip(blocks, pending):
+            if query is not None:
+                following.append(dot(key_rows[block], query, NT))
+            raised.append(jnp.exp(tile - highest).astype(BF16))
+        mixed = dot(value_parts[step], jnp.concatenate(raised, axis=0), NN)
+        totals = mixed[HEAD_WIDTH : HEAD_WIDTH + 1]
+        put(step, mixed[:HEAD_WIDTH] / totals, highest + jnp.log(totals))
         pending = following
 
 
@@ -240,10 +279,11 @@
     )[0]
 
 
-def far_kernel(r_ref, *refs):
-    m_ref, s_ref = refs[-2:]
+def far_kernel(r_ref, others_ref, m_ref, s_ref, stage_ref, sems):
+    early = pltpu.make_async_copy(m_ref, s_ref.at[:, 0:BACK_MID, :], sems.at[0])
+    early.start()
     queries = r_ref[:, MID + MID // 2 : SEND_MID, :].astype(F32) * SCALE
-    others = jnp.concatenate([ref[...] for ref in refs[:-2]], axis=0).astype(F32)
+    others = others_ref[...].astype(F32)
     count = SEG * FAR
     low = lane_low((count, LANES))
     lane = lax.broadcasted_iota(jnp.int32, (count, LANES), 1)
@@ -273,14 +313,27 @@
                 )
         pieces.append(jnp.where(low, outs[0], outs[1]).reshape(SEG, FAR, LANES))
     pieces.append(marks.reshape(SEG, FAR, LANES))
-    s_ref[:, BACK_MID:, :] = jnp.concatenate(pieces, axis=1).astype(BF16)
-    s_ref[:, :BACK_MID, :] = m_ref[...]
+    stage_ref[...] = jnp.concatenate(pieces, axis=1).astype(BF16)
+    late = pltpu.make_async_copy(stage_ref, s_ref.at[:, BACK_MID:BACK, :], sems.at[1])
+    late.start()
+    early.wait()
+    late.wait()
 
 
 def far(received, others, mid_part):
-    return held_call(
-        far_kernel, [((SEG, BACK, LANES), BF16)], received, *others, mid_part, name="far"
-    )[0]
+    operands = (received, others, mid_part)
+    return pl.pallas_call(
+        far_kernel,
+        out_shape=jax.ShapeDtypeStruct((SEG, BACK, LANES), BF16),
+        in_specs=[pl.BlockSpec(memory_space=pltpu.VMEM)] * len(operands),
+        out_specs=pl.BlockSpec(memory_space=pl.ANY),
+        scratch_shapes=[
+            pltpu.VMEM((SEG, BACK - BACK_MID, LANES), BF16),
+            pltpu.SemaphoreType.DMA((2,)),
+        ],
+        compiler_params=pltpu.CompilerParams(vmem_limit_bytes=8 * 2**20),
+        name="far",
+    )(*[pltpu.with_memory_space_constraint(x, pltpu.VMEM) for x in operands])
 
 
 def merge_kernel(*refs):
@@ -390,25 +443,23 @@
     )(*[pltpu.with_memory_space_constraint(x, pltpu.VMEM) for x in operands])
 
 
-def fan_out(held, masks):
+def body(queries, keys, values):
     size = lax.axis_size("grp")
-    got = []
-    for mask in masks:
-        got.append(lax.ppermute(held, "grp", [(i, i ^ mask) for i in range(size)]))
-    return got
-
-
-def body(queries, keys, values):
-    mid_send, held, *pieces = pack(queries, keys, values)
+    near_groups = [[first + i for i in range(4)] for first in range(0, size, 4)]
+    held = pack_far(keys, values)
+    mid_send, *pieces = pack(queries, keys, values)
     mid_got = lax.all_to_all(mid_send, "seg", 0, 0, tiled=True)
     for mask in (8, 4):
-        held = jnp.concatenate([held] + fan_out(held, (mask,)), axis=0)
-    inner = fan_out(held, (1, 3, 2))
+        other = lax.ppermute(held, "grp", [(i, i ^ mask) for i in range(size)])
+        held = jnp.concatenate([held, other], axis=0)
+    others = lax.all_to_all(
+        jnp.tile(held, (4, 1, 1)), "grp", 0, 0, tiled=True, axis_index_groups=near_groups
+    )
     nears = []
     for pair in range(3):
         nears.append(near(*pieces[3 * pair : 3 * pair + 3]))
     mid_part = mid(mid_got)
-    part = far(mid_got, (held, *inner), mid_part)
+    part = far(mid_got, others, mid_part)
     back = lax.all_to_all(part, "seg", 0, 0, tiled=True)
     return merge([n[0] for n in nears], [n[1] for n in nears], back)
 

time: 75.1 us -> 70.3 us (0.936)
  starting transfers between devices: 42 us -> 36.8 us
  Pallas kernels: 19.6 us -> 18.1 us
  waiting for transfers between devices: 12.6 us -> 13.8 us
    ppermute x5 -> x2, starting transfers between devices: 23.2 us -> 14.1 us  [body(): other = lax.ppermute(held, 'grp', [(i, i ^ mask) for i in range(size)])]
    pallas_call x5 -> x4, Pallas kernels: 15 us -> 10.5 us  [held_call(): pl.pallas_call(kernel, out_shape=outs, in_specs=[space] * len(operands),...]
    all_to_all x0 -> x1, starting transfers between devices: none -> 4.18 us  [body(): lax.all_to_all(jnp.tile(held, (4, 1, 1)), 'grp', 0, 0, tiled=True, axis_i...]
    all_to_all x0 -> x1, waiting for transfers between devices: none -> 3.52 us  [body(): lax.all_to_all(jnp.tile(held, (4, 1, 1)), 'grp', 0, 0, tiled=True, axis_i...]
    pallas_call x0 -> x2, Pallas kernels: none -> 3.04 us  [the longest x1 2.17 us: far(): pl.pallas_call(far_kernel, out_shape=jax.ShapeDtypeStruct((SEG, BACK, LAN...]
    ppermute x5 -> x2, waiting for transfers between devices: 12.6 us -> 10.3 us  [body(): other = lax.ppermute(held, 'grp', [(i, i ^ mask) for i in range(size)])]
  transfers between devices with their start and end apart: 7 -> 5, of which waited for: 3 -> 3; matrix products, arithmetic and copies ran while one was open for 0% -> 0% of each run, Pallas kernels for 17% -> 16%
where the time goes in v3:
time: 70.3 us; the launch traced here: 69.8 us
  starting transfers between devices  36.8 us (52%)
  Pallas kernels  18.1 us (26%)
  waiting for transfers between devices  13.8 us (20%)
    ppermute x2, starting transfers between devices, body(): other = lax.ppermute(held, 'grp', [(i, i ^ mask) for i in range(size)])  14.1 us
    pallas_call x4, Pallas kernels, held_call(): pl.pallas_call(kernel, out_shape=outs, in_specs=[space] * len(operands),...  10.5 us
    ppermute x2, waiting for transfers between devices, body(): other = lax.ppermute(held, 'grp', [(i, i ^ mask) for i in range(size)])  10.3 us
    all_to_all x1, starting transfers between devices, body(): mid_got = lax.all_to_all(mid_send, 'seg', 0, 0, tiled=True)  10.2 us
    all_to_all x1, starting transfers between devices, body(): back = lax.all_to_all(part, 'seg', 0, 0, tiled=True)  8.31 us
    all_to_all x1, starting transfers between devices, body(): lax.all_to_all(jnp.tile(held, (4, 1, 1)), 'grp', 0, 0, tiled=True, axis_i...  4.18 us
    all_to_all x1, waiting for transfers between devices, body(): lax.all_to_all(jnp.tile(held, (4, 1, 1)), 'grp', 0, 0, tiled=True, axis_i...  3.52 us
    pallas_call x1, Pallas kernels, pack(): pl.pallas_call(pack_kernel, out_shape=tuple((pltpu.VMEM(shape, dtype) for...  2.57 us
  transfers between devices with their start and end apart: 5, of which 3 were waited for; matrix products, arithmetic and copies ran while one was open for 0% of the time, Pallas kernels for 16%

profile of v3, /device:TPU:1, one launch (start us, length us, event | category | flops | bytes accessed | tf_op | source)
XLA Modules:
  0.0 69.8 jit_solution(1341302220266629545)
XLA Ops:
  0.0 2.6 %pack.1 = (bf16[8,216,128]{2,1,0:T(8,128)(2,1)}, bf16[1024,128]{1,0:T(8,128)(2,1)S(1)}, bf16[1024,128]{1,0:T(8,128)(2,1)S(1)}, bf16[1024,128]{1,0:T(8,128)(2,1)S...) custom-call(bf16[1024,384]{1,0:T(8,128)(2,1)} %refs_0_.1, ...), custom_call_target="tpu_custom_call" | custom-call | tf_op jit(solution)/shard_map/pack/pallas_call | solution.py:150
  2.6 10.2 %all-to-all-start = ((bf16[8,216,128]{2,1,0:T(8,128)(2,1)}), bf16[8,216,128]{2,1,0:T(8,128)(2,1)S(1)}, u32[]{:S(2)}, u32[]{:S(2)}) async-start(bf16[8,216,128]{2,1,0:T(8,128)(2,1)} %get-tuple-element.36), calls=%async_computation | async-start | bytes 884736 | tf_op jit(solution)/shard_map/all_to_all | solution.py:451
  12.8 0.9 %pack_far.1 = bf16[1,48,128]{2,1,0:T(8,128)(2,1)S(1)} custom-call(bf16[8,128,384]{2,1,0:T(8,128)(2,1)} %bitcast.3, bf16[8,128,384]{2,1,0:T(8,128)(2,1)} %bitcast.4), custom_call_target="tpu_custom_call" | custom-call | tf_op jit(solution)/shard_map/pack_far/pallas_call | solution.py:85
  13.7 10.1 %collective-permute-start = (bf16[1,48,128]{2,1,0:T(8,128)(2,1)S(1)}, bf16[1,48,128]{2,1,0:T(8,128)(2,1)S(1)}, u32[]{:S(2)}, u32[]{:S(2)}) collective-permute-start(bf16[1,48,128]{2,1,0:T(8,128)(2,1)S(1)} %pack_far.1), channel_id=1, source_target_pairs={{0,64},{8,72},{16,80},{24,88},{32,96},{40,104},{48,112},{56,120},{... | collective-permute-start | bytes 36872 | tf_op jit(solution)/shard_map/ppermute | solution.py:453
  23.8 5.6 %collective-permute-done = bf16[1,48,128]{2,1,0:T(8,128)(2,1)S(1)} collective-permute-done((bf16[1,48,128]{2,1,0:T(8,128)(2,1)S(1)}, bf16[1,48,128]{2,1,0:T(8,128)(2,1)S(1)}, u32[]{:S(2)}, u32[]{:S(2)}) %collective-permute-start) | collective-permute-done | bytes 12320 | tf_op jit(solution)/shard_map/ppermute | solution.py:453
  29.4 4.0 %collective-permute-start.1 = (bf16[2,48,128]{2,1,0:T(8,128)(2,1)S(1)}, bf16[2,48,128]{2,1,0:T(8,128)(2,1)S(1)}, u32[]{:S(2)}, u32[]{:S(2)}) collective-permute-start(bf16[2,48,128]{2,1,0:T(8,128)(2,1)S(1)} %pad_maximum_fusion.1), channel_id=1, source_target_pairs={{0,32},{8,40},{16,48},{24,56},{32,0},{40,8},{48,16},{56,24},{64,96... | collective-permute-start | bytes 73736 | tf_op jit(solution)/shard_map/ppermute | solution.py:453
  33.4 4.7 %collective-permute-done.1 = bf16[2,48,128]{2,1,0:T(8,128)(2,1)S(1)} collective-permute-done((bf16[2,48,128]{2,1,0:T(8,128)(2,1)S(1)}, bf16[2,48,128]{2,1,0:T(8,128)(2,1)S(1)}, u32[]{:S(2)}, u32[]{:S(2)}) %collective-permute-start.1) | collective-permute-done | bytes 24608 | tf_op jit(solution)/shard_map/ppermute | solution.py:453
  38.1 0.0 all-to-all-done.r_ref
  38.1 0.7 %tile.4 = bf16[4,4,48,128]{3,2,1,0:T(8,128)(2,1)} broadcast(bf16[4,48,128]{2,1,0:T(8,128)(2,1)S(1)} %pad_maximum_fusion), dimensions={1,2,3} | broadcast | bytes 245760 | tf_op jit(solution)/shard_map/tile | solution.py:456
  38.8 4.2 %all-to-all-start.1 = ((bf16[16,48,128]{2,1,0:T(8,128)(2,1)}), bf16[16,48,128]{2,1,0:T(8,128)(2,1)S(1)}, u32[]{:S(2)}, u32[]{:S(2)}) async-start(bf16[16,48,128]{2,1,0:T(8,128)(2,1)} %bitcast.2), calls=%async_computation.1 | async-start | bytes 393216 | tf_op jit(solution)/shard_map/all_to_all | solution.py:455
  43.0 1.7 %mid.1.m_ref = bf16[8,72,128]{2,1,0:T(8,128)(2,1)S(1)} custom-call(bf16[8,216,128]{2,1,0:T(8,128)(2,1)S(1)} %all-to-all-done.r_ref), custom_call_target="tpu_custom_call" | custom-call | flops 268435456 | bytes 524288 | tf_op jit(solution)/shard_map/mid/pallas_call | solution.py:37
  44.7 3.5 %all-to-all-done.1.others_ref = bf16[16,48,128]{2,1,0:T(8,128)(2,1)S(1)} async-done(((bf16[16,48,128]{2,1,0:T(8,128)(2,1)}), bf16[16,48,128]{2,1,0:T(8,128)(2,1)S(1)}, u32[]{:S(2)}, u32[]{:S(2)}) %all-to-all-start.1) | async-done | bytes 196640 | tf_op jit(solution)/shard_map/all_to_all | solution.py:455
  48.2 2.2 %far.1 = bf16[8,104,128]{2,1,0:T(8,128)(2,1)} custom-call(bf16[8,216,128]{2,1,0:T(8,128)(2,1)S(1)} %all-to-all-done.r_ref, bf16[16,48,128]{2,1,0:T(8,128)(2,1)S(1)} %all-to-all-done.1.others_ref, bf16[8,72,128]{2,1,0:T(8,128)(2,1)S(1)} %mid.1.m_ref), custom_call_target="tpu_custom_call" | custom-call | tf_op jit(solution)/shard_map/far/pallas_call | solution.py:325
  50.4 8.3 %all-to-all-start.2 = ((bf16[8,104,128]{2,1,0:T(8,128)(2,1)}), bf16[8,104,128]{2,1,0:T(8,128)(2,1)S(1)}, u32[]{:S(2)}, u32[]{:S(2)}) async-start(bf16[8,104,128]{2,1,0:T(8,128)(2,1)} %far.1), calls=%async_computation.2 | async-start | bytes 425984 | tf_op jit(solution)/shard_map/all_to_all | solution.py:463
  58.7 2.9 %near.3 = (bf16[128,1024]{1,0:T(8,128)(2,1)S(1)}, f32[1,8,1024]{2,1,0:T(8,128)S(1)}) custom-call(bf16[1024,128]{1,0:T(8,128)(2,1)S(1)} %get-tuple-element.21.q_ref, bf16[1024,128]{1,0:T(8,128)(2,1)S(1)} %get-tuple-element.22.k_ref, bf16[1024,128]{1,0:T(8,128)(2,1)S(1)} %get-tuple-element.23.v_ref), custom_call_target="tpu_custom_call" | custom-call | flops 536870912 | bytes 1048576 | tf_op jit(solution)/shard_map/near/pallas_call | solution.py:37
  61.6 3.0 %near.4 = (bf16[128,1024]{1,0:T(8,128)(2,1)S(1)}, f32[1,8,1024]{2,1,0:T(8,128)S(1)}) custom-call(bf16[1024,128]{1,0:T(8,128)(2,1)S(1)} %get-tuple-element.25.q_ref, bf16[1024,128]{1,0:T(8,128)(2,1)S(1)} %get-tuple-element.26.k_ref, bf16[1024,128]{1,0:T(8,128)(2,1)S(1)} %get-tuple-element.27.v_ref), custom_call_target="tpu_custom_call" | custom-call | flops 536870912 | bytes 1048576 | tf_op jit(solution)/shard_map/near/pallas_call | solution.py:37
  64.6 3.0 %near.5 = (bf16[128,1024]{1,0:T(8,128)(2,1)S(1)}, f32[1,8,1024]{2,1,0:T(8,128)S(1)}) custom-call(bf16[1024,128]{1,0:T(8,128)(2,1)S(1)} %get-tuple-element.29.q_ref, bf16[1024,128]{1,0:T(8,128)(2,1)S(1)} %get-tuple-element.30.k_ref, bf16[1024,128]{1,0:T(8,128)(2,1)S(1)} %get-tuple-element.31.v_ref), custom_call_target="tpu_custom_call" | custom-call | flops 536870912 | bytes 1048576 | tf_op jit(solution)/shard_map/near/pallas_call | solution.py:37
  67.6 0.0 all-to-all-done.2.refs_6_
  67.6 2.0 %merge.1 = bf16[1024,384]{1,0:T(8,128)(2,1)} custom-call(bf16[128,1024]{1,0:T(8,128)(2,1)S(1)} %get-tuple-element.24.refs_0_, bf16[128,1024]{1,0:T(8,128)(2,1)S(1)} %get-tuple-element.28.refs_1_, bf16[128,1024]{1,0:T(8,128)(2,1)S(1)} %get-tuple-element.32.refs_2_, f32[1,8,1024]{2,1,0:T(8,128)S(1)} %get-tuple-element.33.refs_3_, ...), custom_call_target="tpu_custom_call" | custom-call | tf_op jit(solution)/shard_map/merge/pallas_call | solution.py:432
  (2 shorter events, 0.0 us)
Async XLA Ops:
  2.6 35.5 %all-to-all-start = ((bf16[8,216,128]{2,1,0:T(8,128)(2,1)}), bf16[8,216,128]{2,1,0:T(8,128)(2,1)S(1)}, u32[]{:S(2)}, u32[]{:S(2)}) async-start(bf16[8,216,128]{2,1,0:T(8,128)(2,1)} %get-tuple-element.36), calls=%async_computation | async-start | bytes 884736 | tf_op jit(solution)/shard_map/all_to_all | solution.py:451
  13.7 15.7 %collective-permute-start = (bf16[1,48,128]{2,1,0:T(8,128)(2,1)S(1)}, bf16[1,48,128]{2,1,0:T(8,128)(2,1)S(1)}, u32[]{:S(2)}, u32[]{:S(2)}) collective-permute-start(bf16[1,48,128]{2,1,0:T(8,128)(2,1)S(1)} %pack_far.1), channel_id=1, source_target_pairs={{0,64},{8,72},{16,80},{24,88},{32,96},{40,104},{48,112},{56,120},{... | collective-permute-start | bytes 36872 | tf_op jit(solution)/shard_map/ppermute | solution.py:453
  29.4 8.7 %collective-permute-start.1 = (bf16[2,48,128]{2,1,0:T(8,128)(2,1)S(1)}, bf16[2,48,128]{2,1,0:T(8,128)(2,1)S(1)}, u32[]{:S(2)}, u32[]{:S(2)}) collective-permute-start(bf16[2,48,128]{2,1,0:T(8,128)(2,1)S(1)} %pad_maximum_fusion.1), channel_id=1, source_target_pairs={{0,32},{8,40},{16,48},{24,56},{32,0},{40,8},{48,16},{56,24},{64,96... | collective-permute-start | bytes 73736 | tf_op jit(solution)/shard_map/ppermute | solution.py:453
  38.8 9.4 %all-to-all-start.1 = ((bf16[16,48,128]{2,1,0:T(8,128)(2,1)}), bf16[16,48,128]{2,1,0:T(8,128)(2,1)S(1)}, u32[]{:S(2)}, u32[]{:S(2)}) async-start(bf16[16,48,128]{2,1,0:T(8,128)(2,1)} %bitcast.2), calls=%async_computation.1 | async-start | bytes 393216 | tf_op jit(solution)/shard_map/all_to_all | solution.py:455
  50.4 17.2 %all-to-all-start.2 = ((bf16[8,104,128]{2,1,0:T(8,128)(2,1)}), bf16[8,104,128]{2,1,0:T(8,128)(2,1)S(1)}, u32[]{:S(2)}, u32[]{:S(2)}) async-start(bf16[8,104,128]{2,1,0:T(8,128)(2,1)} %far.1), calls=%async_computation.2 | async-start | bytes 425984 | tf_op jit(solution)/shard_map/all_to_all | solution.py:463

commit v4 on v3

--- a/solution.py
+++ b/solution.py
@@ -287,31 +287,36 @@
     count = SEG * FAR
     low = lane_low((count, LANES))
     lane = lax.broadcasted_iota(jnp.int32, (count, LANES), 1)
-    marks = jnp.zeros((count, LANES), F32)
-    pieces = []
+    tiles, value_sides = [], []
     for pair in range(PAIRS):
         rows = queries[:, pair * FAR : (pair + 1) * FAR, :].reshape(count, LANES)
         key_rows = (
             others[:, pair * FAR : (pair + 1) * FAR, :].reshape(SLIDE_GRP * FAR, LANES).astype(BF16)
         )
-        value_rows = (
+        value_sides.append(
             others[:, (PAIRS + pair) * FAR : (PAIRS + pair + 1) * FAR, :]
             .reshape(SLIDE_GRP * FAR, LANES)
             .astype(BF16)
         )
-        outs = []
+        both = jnp.concatenate([jnp.where(low, rows, 0.0), jnp.where(low, 0.0, rows)], axis=0)
+        tiles.append(dot(both.astype(BF16), key_rows, NT))
+    scores = jnp.concatenate(tiles, axis=0)
+    highest = jnp.max(scores, axis=1, keepdims=True)
+    raised = jnp.exp(scores - highest).astype(BF16)
+    totals = dot(raised, jnp.ones((SLIDE_GRP * FAR, LANES), BF16), NN)
+    parts = [part.astype(F32) for part in split3(highest + jnp.log(totals))]
+    marks = jnp.zeros((count, LANES), F32)
+    pieces = []
+    for pair in range(PAIRS):
+        span = slice(2 * pair * count, 2 * (pair + 1) * count)
+        mixed = dot(raised[span], value_sides[pair], NN) / totals[span]
+        pieces.append(jnp.where(low, mixed[:count], mixed[count:]).reshape(SEG, FAR, LANES))
         for side in range(2):
-            keep = low if side == 0 else jnp.logical_not(low)
-            scores = dot(jnp.where(keep, rows, 0.0).astype(BF16), key_rows, NT)
-            highest = jnp.max(scores, axis=1, keepdims=True)
-            raised = jnp.exp(scores - highest)
-            totals = jnp.sum(raised, axis=1, keepdims=True)
-            outs.append(dot(raised.astype(BF16), value_rows, NN) / totals)
-            for place, part in enumerate(split3(highest + jnp.log(totals))):
+            head = 2 * pair + side
+            for place, part in enumerate(parts):
                 marks = jnp.where(
-                    lane == 3 * (2 * pair + side) + place, part.astype(F32), marks
+                    lane == 3 * head + place, part[head * count : (head + 1) * count], marks
                 )
-        pieces.append(jnp.where(low, outs[0], outs[1]).reshape(SEG, FAR, LANES))
     pieces.append(marks.reshape(SEG, FAR, LANES))
     stage_ref[...] = jnp.concatenate(pieces, axis=1).astype(BF16)
     late = pltpu.make_async_copy(stage_ref, s_ref.at[:, BACK_MID:BACK, :], sems.at[1])
@@ -336,9 +341,20 @@
     )(*[pltpu.with_memory_space_constraint(x, pltpu.VMEM) for x in operands])
 
 
+def maps_kernel(o_ref):
+    slot = lax.broadcasted_iota(jnp.int32, (MID, ROWS), 0) * SEG
+    offset = lax.broadcasted_iota(jnp.int32, (MID, ROWS), 1) - slot
+    for head in range(HEADS):
+        o_ref[head] = (offset == head).astype(BF16)
+
+
+def maps():
+    return held_call(maps_kernel, [((HEADS, MID, ROWS), BF16)], name="maps")[0]
+
+
 def merge_kernel(*refs):
     near_refs, lse_refs = refs[:PAIRS], refs[PAIRS : 2 * PAIRS]
-    back_ref, out_ref, stage_ref, sems = refs[2 * PAIRS :]
+    back_ref, map_ref, out_ref, stage_ref, sems = refs[2 * PAIRS :]
     moves = []
     width = HEADS * HEAD_WIDTH
     parts = back_ref[:, BACK_MID:, :].astype(F32)
@@ -366,9 +382,6 @@
     far_rows = jnp.concatenate([far_out] + [x.astype(F32) for x in split3(far_lse)], axis=1)
     far_wide = dot(far_rows.astype(BF16), thin, TN)
     has_far = lax.broadcasted_iota(jnp.int32, (1, MID), 1) % (MID // FAR) == 0
-    slot = lax.broadcasted_iota(jnp.int32, (MID, ROWS), 0) * SEG
-    token = lax.broadcasted_iota(jnp.int32, (MID, ROWS), 1)
-    offset = token - slot
     phase = lax.broadcasted_iota(jnp.int32, (1, ROWS), 1) % SEG
     start = 0
     for ref, lse_ref in zip(near_refs, lse_refs):
@@ -399,7 +412,7 @@
                     + [jnp.zeros((BACK_MID - HEAD_WIDTH - 3, MID), F32)],
                     axis=0,
                 ).astype(BF16)
-                spread = dot(block, (offset == head).astype(BF16), NN)
+                spread = dot(block, map_ref[head], NN)
                 near_lse = lse_ref[pair, side : side + 1, :]
                 joint_wide = spread[64:65] + spread[65:66] + spread[66:67]
                 covered = phase == head
@@ -427,8 +440,8 @@
         move.wait()
 
 
-def merge(near_outs, near_lses, back):
-    operands = (*near_outs, *near_lses, back)
+def merge(near_outs, near_lses, back, places):
+    operands = (*near_outs, *near_lses, back, places)
     return pl.pallas_call(
         merge_kernel,
         out_shape=jax.ShapeDtypeStruct((ROWS, HEADS * HEAD_WIDTH), BF16),
@@ -461,7 +474,8 @@
     mid_part = mid(mid_got)
     part = far(mid_got, others, mid_part)
     back = lax.all_to_all(part, "seg", 0, 0, tiled=True)
-    return merge([n[0] for n in nears], [n[1] for n in nears], back)
+    places = maps()
+    return merge([n[0] for n in nears], [n[1] for n in nears], back, places)
 
 
 def solution(mesh):

time: 70.3 us -> 74.3 us (1.057)
  local copies, waits for them, and re-layouts: 0.7 us -> 5.37 us
    unnamed x0 -> x16, local copies, waits for them, and re-layouts: none -> 4.66 us
    pallas_call x1, Pallas kernels: 2.17 us -> 1.13 us  [far(): pl.pallas_call(far_kernel, out_shape=jax.ShapeDtypeStruct((SEG, BACK, LAN...]
    pallas_call x4 -> x5, Pallas kernels: 10.5 us -> 10.8 us  [held_call(): pl.pallas_call(kernel, out_shape=outs, in_specs=[space] * len(operands),...]
where the time goes in v4:
time: 74.3 us; the launch traced here: 73.7 us
  starting transfers between devices  36.8 us (50%)
  Pallas kernels  17.4 us (23%)
  waiting for transfers between devices  13.9 us (19%)
  local copies, waits for them, and re-layouts  5.37 us (7%)
    ppermute x2, starting transfers between devices, body(): other = lax.ppermute(held, 'grp', [(i, i ^ mask) for i in range(size)])  14.1 us
    pallas_call x5, Pallas kernels, held_call(): pl.pallas_call(kernel, out_shape=outs, in_specs=[space] * len(operands),...  10.8 us
    ppermute x2, waiting for transfers between devices, body(): other = lax.ppermute(held, 'grp', [(i, i ^ mask) for i in range(size)])  10.3 us
    all_to_all x1, starting transfers between devices, body(): mid_got = lax.all_to_all(mid_send, 'seg', 0, 0, tiled=True)  10.2 us
    all_to_all x1, starting transfers between devices, body(): back = lax.all_to_all(part, 'seg', 0, 0, tiled=True)  8.31 us
    unnamed x16, local copies, waits for them, and re-layouts  4.66 us
    all_to_all x1, starting transfers between devices, body(): lax.all_to_all(jnp.tile(held, (4, 1, 1)), 'grp', 0, 0, tiled=True, axis_i...  4.18 us
    all_to_all x1, waiting for transfers between devices, body(): lax.all_to_all(jnp.tile(held, (4, 1, 1)), 'grp', 0, 0, tiled=True, axis_i...  3.53 us
  transfers between devices with their start and end apart: 5, of which 3 were waited for; matrix products, arithmetic and copies ran while one was open for 0% of the time, Pallas kernels for 16%

profile of v4, /device:TPU:1, one launch (start us, length us, event | category | flops | bytes accessed | tf_op | source)
XLA Modules:
  0.0 73.7 jit_solution(648017413468840082)
XLA Ops:
  0.0 2.6 %pack.1 = (bf16[8,216,128]{2,1,0:T(8,128)(2,1)}, bf16[1024,128]{1,0:T(8,128)(2,1)S(1)}, bf16[1024,128]{1,0:T(8,128)(2,1)S(1)}, bf16[1024,128]{1,0:T(8,128)(2,1)S...) custom-call(bf16[1024,384]{1,0:T(8,128)(2,1)} %refs_0_.1, ...), custom_call_target="tpu_custom_call" | custom-call | tf_op jit(solution)/shard_map/pack/pallas_call | solution.py:150
  2.6 0.0 copy-start
  2.6 0.7 copy-done
  3.3 0.0 copy-start.2
  3.3 0.7 copy-done.2
  4.0 0.0 copy-start.4
  4.0 0.7 copy-done.4
  4.7 0.7 copy-done.6
  5.4 10.2 %all-to-all-start = ((bf16[8,216,128]{2,1,0:T(8,128)(2,1)}), bf16[8,216,128]{2,1,0:T(8,128)(2,1)S(1)}, u32[]{:S(2)}, u32[]{:S(2)}) async-start(bf16[8,216,128]{2,1,0:T(8,128)(2,1)} %get-tuple-element.36), calls=%async_computation | async-start | bytes 884736 | tf_op jit(solution)/shard_map/all_to_all | solution.py:464
  15.6 0.9 %pack_far.1 = bf16[1,48,128]{2,1,0:T(8,128)(2,1)S(1)} custom-call(bf16[8,128,384]{2,1,0:T(8,128)(2,1)} %bitcast.3, bf16[8,128,384]{2,1,0:T(8,128)(2,1)} %bitcast.4), custom_call_target="tpu_custom_call" | custom-call | tf_op jit(solution)/shard_map/pack_far/pallas_call | solution.py:85
  16.4 10.1 %collective-permute-start = (bf16[1,48,128]{2,1,0:T(8,128)(2,1)S(1)}, bf16[1,48,128]{2,1,0:T(8,128)(2,1)S(1)}, u32[]{:S(2)}, u32[]{:S(2)}) collective-permute-start(bf16[1,48,128]{2,1,0:T(8,128)(2,1)S(1)} %pack_far.1), channel_id=1, source_target_pairs={{0,64},{8,72},{16,80},{24,88},{32,96},{40,104},{48,112},{56,120},{... | collective-permute-start | bytes 36872 | tf_op jit(solution)/shard_map/ppermute | solution.py:466
  26.5 5.6 %collective-permute-done = bf16[1,48,128]{2,1,0:T(8,128)(2,1)S(1)} collective-permute-done((bf16[1,48,128]{2,1,0:T(8,128)(2,1)S(1)}, bf16[1,48,128]{2,1,0:T(8,128)(2,1)S(1)}, u32[]{:S(2)}, u32[]{:S(2)}) %collective-permute-start) | collective-permute-done | bytes 12320 | tf_op jit(solution)/shard_map/ppermute | solution.py:466
  32.2 4.0 %collective-permute-start.1 = (bf16[2,48,128]{2,1,0:T(8,128)(2,1)S(1)}, bf16[2,48,128]{2,1,0:T(8,128)(2,1)S(1)}, u32[]{:S(2)}, u32[]{:S(2)}) collective-permute-start(bf16[2,48,128]{2,1,0:T(8,128)(2,1)S(1)} %pad_maximum_fusion.1), channel_id=1, source_target_pairs={{0,32},{8,40},{16,48},{24,56},{32,0},{40,8},{48,16},{56,24},{64,96... | collective-permute-start | bytes 73736 | tf_op jit(solution)/shard_map/ppermute | solution.py:466
  36.2 4.7 %collective-permute-done.1 = bf16[2,48,128]{2,1,0:T(8,128)(2,1)S(1)} collective-permute-done((bf16[2,48,128]{2,1,0:T(8,128)(2,1)S(1)}, bf16[2,48,128]{2,1,0:T(8,128)(2,1)S(1)}, u32[]{:S(2)}, u32[]{:S(2)}) %collective-permute-start.1) | collective-permute-done | bytes 24608 | tf_op jit(solution)/shard_map/ppermute | solution.py:466
  40.9 0.0 all-to-all-done.r_ref
  40.9 0.7 tile.4
  41.6 4.2 %all-to-all-start.1 = ((bf16[16,48,128]{2,1,0:T(8,128)(2,1)}), bf16[16,48,128]{2,1,0:T(8,128)(2,1)S(1)}, u32[]{:S(2)}, u32[]{:S(2)}) async-start(bf16[16,48,128]{2,1,0:T(8,128)(2,1)} %bitcast.2), calls=%async_computation.1 | async-start | bytes 393216 | tf_op jit(solution)/shard_map/all_to_all | solution.py:468
  45.8 1.6 %mid.1.m_ref = bf16[8,72,128]{2,1,0:T(8,128)(2,1)S(1)} custom-call(bf16[8,216,128]{2,1,0:T(8,128)(2,1)S(1)} %all-to-all-done.r_ref), custom_call_target="tpu_custom_call" | custom-call | flops 268435456 | bytes 524288 | tf_op jit(solution)/shard_map/mid/pallas_call | solution.py:37
  47.4 3.5 %all-to-all-done.1.others_ref = bf16[16,48,128]{2,1,0:T(8,128)(2,1)S(1)} async-done(((bf16[16,48,128]{2,1,0:T(8,128)(2,1)}), bf16[16,48,128]{2,1,0:T(8,128)(2,1)S(1)}, u32[]{:S(2)}, u32[]{:S(2)}) %all-to-all-start.1) | async-done | bytes 196640 | tf_op jit(solution)/shard_map/all_to_all | solution.py:468
  51.0 1.1 %far.1 = bf16[8,104,128]{2,1,0:T(8,128)(2,1)} custom-call(bf16[8,216,128]{2,1,0:T(8,128)(2,1)S(1)} %all-to-all-done.r_ref, bf16[16,48,128]{2,1,0:T(8,128)(2,1)S(1)} %all-to-all-done.1.others_ref, bf16[8,72,128]{2,1,0:T(8,128)(2,1)S(1)} %mid.1.m_ref), custom_call_target="tpu_custom_call" | custom-call | tf_op jit(solution)/shard_map/far/pallas_call | solution.py:330
  52.1 8.3 %all-to-all-start.2 = ((bf16[8,104,128]{2,1,0:T(8,128)(2,1)}), bf16[8,104,128]{2,1,0:T(8,128)(2,1)S(1)}, u32[]{:S(2)}, u32[]{:S(2)}) async-start(bf16[8,104,128]{2,1,0:T(8,128)(2,1)} %far.1), calls=%async_computation.2 | async-start | bytes 425984 | tf_op jit(solution)/shard_map/all_to_all | solution.py:476
  60.4 0.3 maps.1.refs_7_
  60.7 0.0 copy-start.5
  60.7 0.9 %copy-done.5 = bf16[1024,128]{1,0:T(8,128)(2,1)S(1)} copy-done((bf16[1024,128]{1,0:T(8,128)(2,1)S(1)}, bf16[1024,128]{1,0:T(8,128)(2,1)}, u32[]{:S(2)}) %copy-start.5) | copy-done | bytes 262168
  61.7 0.9 %copy-done.7 = bf16[1024,128]{1,0:T(8,128)(2,1)S(1)} copy-done((bf16[1024,128]{1,0:T(8,128)(2,1)S(1)}, bf16[1024,128]{1,0:T(8,128)(2,1)}, u32[]{:S(2)}) %copy-start.7) | copy-done | bytes 262168
  62.6 3.0 %near.5 = (bf16[128,1024]{1,0:T(8,128)(2,1)S(1)}, f32[1,8,1024]{2,1,0:T(8,128)S(1)}) custom-call(bf16[1024,128]{1,0:T(8,128)(2,1)S(1)} %get-tuple-element.29.q_ref, bf16[1024,128]{1,0:T(8,128)(2,1)S(1)} %copy-done.5, bf16[1024,128]{1,0:T(8,128)(2,1)S(1)} %copy-done.7), custom_call_target="tpu_custom_call" | custom-call | flops 536870912 | bytes 1048576 | tf_op jit(solution)/shard_map/near/pallas_call | solution.py:37
  65.6 0.0 copy-done.1
  65.6 0.0 copy-done.3
  65.6 3.0 %near.4 = (bf16[128,1024]{1,0:T(8,128)(2,1)S(1)}, f32[1,8,1024]{2,1,0:T(8,128)S(1)}) custom-call(bf16[1024,128]{1,0:T(8,128)(2,1)S(1)} %get-tuple-element.25.q_ref, bf16[1024,128]{1,0:T(8,128)(2,1)S(1)} %copy-done.1, bf16[1024,128]{1,0:T(8,128)(2,1)S(1)} %copy-done.3), custom_call_target="tpu_custom_call" | custom-call | flops 536870912 | bytes 1048576 | tf_op jit(solution)/shard_map/near/pallas_call | solution.py:37
  68.6 3.0 %near.3 = (bf16[128,1024]{1,0:T(8,128)(2,1)S(1)}, f32[1,8,1024]{2,1,0:T(8,128)S(1)}) custom-call(bf16[1024,128]{1,0:T(8,128)(2,1)S(1)} %get-tuple-element.21.q_ref, bf16[1024,128]{1,0:T(8,128)(2,1)S(1)} %get-tuple-element.22.k_ref, bf16[1024,128]{1,0:T(8,128)(2,1)S(1)} %get-tuple-element.23.v_ref), custom_call_target="tpu_custom_call" | custom-call | flops 536870912 | bytes 1048576 | tf_op jit(solution)/shard_map/near/pallas_call | solution.py:37
  71.5 0.0 all-to-all-done.2.refs_6_
  71.5 2.0 %merge.1 = bf16[1024,384]{1,0:T(8,128)(2,1)} custom-call(bf16[128,1024]{1,0:T(8,128)(2,1)S(1)} %get-tuple-element.24.refs_0_, bf16[128,1024]{1,0:T(8,128)(2,1)S(1)} %get-tuple-element.28.refs_1_, bf16[128,1024]{1,0:T(8,128)(2,1)S(1)} %get-tuple-element.32.refs_2_, f32[1,8,1024]{2,1,0:T(8,128)S(1)} %get-tuple-element.33.refs_3_, ...), custom_call_target="tpu_custom_call" | custom-call | tf_op jit(solution)/shard_map/merge/pallas_call | solution.py:445
  (6 shorter events, 0.0 us)
Async XLA Ops:
  2.6 0.7 copy-start
  3.3 0.7 copy-start.2
  4.0 0.7 copy-start.4
  4.7 0.7 copy-start.6
  5.4 35.5 %all-to-all-start = ((bf16[8,216,128]{2,1,0:T(8,128)(2,1)}), bf16[8,216,128]{2,1,0:T(8,128)(2,1)S(1)}, u32[]{:S(2)}, u32[]{:S(2)}) async-start(bf16[8,216,128]{2,1,0:T(8,128)(2,1)} %get-tuple-element.36), calls=%async_computation | async-start | bytes 884736 | tf_op jit(solution)/shard_map/all_to_all | solution.py:464
  16.4 15.7 %collective-permute-start = (bf16[1,48,128]{2,1,0:T(8,128)(2,1)S(1)}, bf16[1,48,128]{2,1,0:T(8,128)(2,1)S(1)}, u32[]{:S(2)}, u32[]{:S(2)}) collective-permute-start(bf16[1,48,128]{2,1,0:T(8,128)(2,1)S(1)} %pack_far.1), channel_id=1, source_target_pairs={{0,64},{8,72},{16,80},{24,88},{32,96},{40,104},{48,112},{56,120},{... | collective-permute-start | bytes 36872 | tf_op jit(solution)/shard_map/ppermute | solution.py:466
  32.2 8.7 %collective-permute-start.1 = (bf16[2,48,128]{2,1,0:T(8,128)(2,1)S(1)}, bf16[2,48,128]{2,1,0:T(8,128)(2,1)S(1)}, u32[]{:S(2)}, u32[]{:S(2)}) collective-permute-start(bf16[2,48,128]{2,1,0:T(8,128)(2,1)S(1)} %pad_maximum_fusion.1), channel_id=1, source_target_pairs={{0,32},{8,40},{16,48},{24,56},{32,0},{40,8},{48,16},{56,24},{64,96... | collective-permute-start | bytes 73736 | tf_op jit(solution)/shard_map/ppermute | solution.py:466
  41.6 9.4 %all-to-all-start.1 = ((bf16[16,48,128]{2,1,0:T(8,128)(2,1)}), bf16[16,48,128]{2,1,0:T(8,128)(2,1)S(1)}, u32[]{:S(2)}, u32[]{:S(2)}) async-start(bf16[16,48,128]{2,1,0:T(8,128)(2,1)} %bitcast.2), calls=%async_computation.1 | async-start | bytes 393216 | tf_op jit(solution)/shard_map/all_to_all | solution.py:468
  52.1 19.4 %all-to-all-start.2 = ((bf16[8,104,128]{2,1,0:T(8,128)(2,1)}), bf16[8,104,128]{2,1,0:T(8,128)(2,1)S(1)}, u32[]{:S(2)}, u32[]{:S(2)}) async-start(bf16[8,104,128]{2,1,0:T(8,128)(2,1)} %far.1), calls=%async_computation.2 | async-start | bytes 425984 | tf_op jit(solution)/shard_map/all_to_all | solution.py:476
  60.7 1.0 %copy-start.5 = (bf16[1024,128]{1,0:T(8,128)(2,1)S(1)}, bf16[1024,128]{1,0:T(8,128)(2,1)}, u32[]{:S(2)}) copy-start(bf16[1024,128]{1,0:T(8,128)(2,1)} %copy-done.4) | copy-start | bytes 786436
  61.7 0.9 %copy-start.7 = (bf16[1024,128]{1,0:T(8,128)(2,1)S(1)}, bf16[1024,128]{1,0:T(8,128)(2,1)}, u32[]{:S(2)}) copy-start(bf16[1024,128]{1,0:T(8,128)(2,1)} %copy-done.6) | copy-start | bytes 786436
  62.6 3.0 %copy-start.1 = (bf16[1024,128]{1,0:T(8,128)(2,1)S(1)}, bf16[1024,128]{1,0:T(8,128)(2,1)}, u32[]{:S(2)}) copy-start(bf16[1024,128]{1,0:T(8,128)(2,1)} %copy-done) | copy-start | bytes 786436
  62.6 3.0 %copy-start.3 = (bf16[1024,128]{1,0:T(8,128)(2,1)S(1)}, bf16[1024,128]{1,0:T(8,128)(2,1)}, u32[]{:S(2)}) copy-start(bf16[1024,128]{1,0:T(8,128)(2,1)} %copy-done.2) | copy-start | bytes 786436

commit v5 on v4

--- a/solution.py
+++ b/solution.py
@@ -60,46 +60,10 @@
     return high, middle, low
 
 
-def pack_far_kernel(k_ref, v_ref, far_ref, taken, wide, sems):
-    moves = []
-    for place, source in enumerate((k_ref, v_ref)):
-        move = pltpu.make_async_copy(source.at[:, 0:SEG, :], taken.at[place], sems.at[place])
-        move.start()
-        moves.append(move)
-    low = lane_low((FAR, LANES))
-    rows = []
-    for place, move in enumerate(moves):
-        move.wait()
-        for pair in range(PAIRS):
-            lanes = slice(pair * LANES, (pair + 1) * LANES)
-            wide[...] = taken[place, :, :, lanes].astype(F32).reshape(FAR * SEG, LANES)
-            first = wide[pl.ds(2 * pair, FAR, stride=SEG), :]
-            second = wide[pl.ds(2 * pair + 1, FAR, stride=SEG), :]
-            rows.append(jnp.where(low, first, second))
-    far_ref[0] = jnp.concatenate(rows, axis=0).astype(BF16)
-
-
-def pack_far(keys, values):
-    width = HEADS * HEAD_WIDTH
-    operands = [x.reshape(FAR, FAR_PERIOD, width) for x in (keys, values)]
-    return pl.pallas_call(
-        pack_far_kernel,
-        out_shape=pltpu.VMEM((1, 2 * PAIRS * FAR, LANES), BF16),
-        in_specs=[pl.BlockSpec(memory_space=pl.ANY)] * 2,
-        out_specs=pl.BlockSpec(memory_space=pltpu.VMEM),
-        scratch_shapes=[
-            pltpu.VMEM((2, FAR, SEG, width), BF16),
-            pltpu.VMEM((FAR * SEG, LANES), F32),
-            pltpu.SemaphoreType.DMA((2,)),
-        ],
-        compiler_params=pltpu.CompilerParams(vmem_limit_bytes=4 * 2**20),
-        name="pack_far",
-    )(*[pltpu.with_memory_space_constraint(x, pltpu.HBM) for x in operands])
-
-
 def pack_kernel(*refs):
     sources, refs = refs[:3], refs[3:]
-    mid_ref, copies, (q_wide, k_wide, v_wide, sems) = refs[0], refs[1:-4], refs[-4:]
+    mid_ref, far_ref = refs[:2]
+    copies, (q_wide, k_wide, v_wide, sems) = refs[2:-4], refs[-4:]
     moves = []
     for pair in range(PAIRS):
         for place, source in enumerate(sources):
@@ -109,7 +73,7 @@
             )
             move.start()
             moves.append(move)
-    far_q = []
+    far_q, far_k, far_v = [], [], []
     low_mid = lane_low((MID, LANES))
     low_half = lane_low((MID // 2, LANES))
     low_far = lane_low((FAR, LANES))
@@ -136,16 +100,19 @@
                 )
             mid_ref[head, 0:MID, :] = key_value.astype(BF16)
             mid_ref[head, MID : MID + MID // 2, :] = query.astype(BF16)
-        first = q_wide[pl.ds(2 * pair, FAR, stride=FAR_PERIOD), :]
-        second = q_wide[pl.ds(2 * pair + 1, FAR, stride=FAR_PERIOD), :]
-        far_q.append(jnp.where(low_far, first, second))
+        for wide, out in ((q_wide, far_q), (k_wide, far_k), (v_wide, far_v)):
+            first = wide[pl.ds(2 * pair, FAR, stride=FAR_PERIOD), :]
+            second = wide[pl.ds(2 * pair + 1, FAR, stride=FAR_PERIOD), :]
+            out.append(jnp.where(low_far, first, second))
     tail = jnp.concatenate(far_q, axis=0).astype(BF16)
     for target in range(SEG):
         mid_ref[target, MID + MID // 2 : SEND_MID, :] = tail
+    far_ref[0] = jnp.concatenate(far_k + far_v, axis=0).astype(BF16)
 
 
 def pack(queries, keys, values):
-    shapes = [((SEG, SEND_MID, LANES), BF16)] + [((ROWS, LANES), BF16)] * (3 * PAIRS)
+    shapes = [((SEG, SEND_MID, LANES), BF16), ((1, 2 * PAIRS * FAR, LANES), BF16)]
+    shapes += [((ROWS, LANES), BF16)] * (3 * PAIRS)
     space = pl.BlockSpec(memory_space=pltpu.VMEM)
     return pl.pallas_call(
         pack_kernel,
@@ -459,8 +426,7 @@
 def body(queries, keys, values):
     size = lax.axis_size("grp")
     near_groups = [[first + i for i in range(4)] for first in range(0, size, 4)]
-    held = pack_far(keys, values)
-    mid_send, *pieces = pack(queries, keys, values)
+    mid_send, held, *pieces = pack(queries, keys, values)
     mid_got = lax.all_to_all(mid_send, "seg", 0, 0, tiled=True)
     for mask in (8, 4):
         other = lax.ppermute(held, "grp", [(i, i ^ mask) for i in range(size)])

time: 74.3 us -> 73.5 us (0.989)
  waiting for transfers between devices: 13.9 us -> 15 us
  Pallas kernels: 17.4 us -> 16.5 us
    ppermute x2, waiting for transfers between devices: 10.3 us -> 11.5 us  [body(): other = lax.ppermute(held, 'grp', [(i, i ^ mask) for i in range(size)])]
    pallas_call x1 -> x0, Pallas kernels: 0.87 us -> none  [pack_far(): pl.pallas_call(pack_far_kernel, out_shape=pltpu.VMEM((1, 2 * PAIRS * FAR,...]
  transfers between devices with their start and end apart: 5 -> 5, of which waited for: 3 -> 3; matrix products, arithmetic and copies ran while one was open for 0% -> 0% of each run, Pallas kernels for 16% -> 15%
where the time goes in v5:
time: 73.5 us; the launch traced here: 73 us
  starting transfers between devices  36.5 us (50%)
  Pallas kernels  16.5 us (22%)
  waiting for transfers between devices  15 us (20%)
  local copies, waits for them, and re-layouts  4.67 us (6%)
    ppermute x2, starting transfers between devices, body(): other = lax.ppermute(held, 'grp', [(i, i ^ mask) for i in range(size)])  14.1 us
    ppermute x2, waiting for transfers between devices, body(): other = lax.ppermute(held, 'grp', [(i, i ^ mask) for i in range(size)])  11.5 us
    pallas_call x5, Pallas kernels, held_call(): pl.pallas_call(kernel, out_shape=outs, in_specs=[space] * len(operands),...  10.8 us
    all_to_all x1, starting transfers between devices, body(): mid_got = lax.all_to_all(mid_send, 'seg', 0, 0, tiled=True)  10.2 us
    all_to_all x1, starting transfers between devices, body(): back = lax.all_to_all(part, 'seg', 0, 0, tiled=True)  8.3 us
    unnamed x16, local copies, waits for them, and re-layouts  3.97 us
    all_to_all x1, starting transfers between devices, body(): lax.all_to_all(jnp.tile(held, (4, 1, 1)), 'grp', 0, 0, tiled=True, axis_i...  3.92 us
    all_to_all x1, waiting for transfers between devices, body(): lax.all_to_all(jnp.tile(held, (4, 1, 1)), 'grp', 0, 0, tiled=True, axis_i...  3.52 us
  transfers between devices with their start and end apart: 5, of which 3 were waited for; matrix products, arithmetic and copies ran while one was open for 0% of the time, Pallas kernels for 15%

profile of v5, /device:TPU:1, one launch (start us, length us, event | category | flops | bytes accessed | tf_op | source)
XLA Modules:
  0.0 73.0 jit_solution(12206275375816494671)
XLA Ops:
  0.0 2.6 %pack.1 = (bf16[8,216,128]{2,1,0:T(8,128)(2,1)}, bf16[1,48,128]{2,1,0:T(8,128)(2,1)S(1)}, bf16[1024,128]{1,0:T(8,128)(2,1)S(1)}, bf16[1024,128]{1,0:T(8,128)(2,1...) custom-call(bf16[1024,384]{1,0:T(8,128)(2,1)} %refs_0_.1, ...), custom_call_target="tpu_custom_call" | custom-call | tf_op jit(solution)/shard_map/pack/pallas_call | solution.py:117
  2.6 0.0 copy-start
  2.6 0.7 copy-done
  3.3 0.0 copy-start.2
  3.3 0.7 copy-done.2
  4.0 0.0 copy-start.4
  4.0 0.7 copy-done.4
  4.7 0.0 copy-start.6
  4.7 10.2 %all-to-all-start = ((bf16[8,216,128]{2,1,0:T(8,128)(2,1)}), bf16[8,216,128]{2,1,0:T(8,128)(2,1)S(1)}, u32[]{:S(2)}, u32[]{:S(2)}) async-start(bf16[8,216,128]{2,1,0:T(8,128)(2,1)} %get-tuple-element.37), calls=%async_computation | async-start | bytes 884736 | tf_op jit(solution)/shard_map/all_to_all | solution.py:430
  14.9 10.1 %collective-permute-start = (bf16[1,48,128]{2,1,0:T(8,128)(2,1)S(1)}, bf16[1,48,128]{2,1,0:T(8,128)(2,1)S(1)}, u32[]{:S(2)}, u32[]{:S(2)}) collective-permute-start(bf16[1,48,128]{2,1,0:T(8,128)(2,1)S(1)} %get-tuple-element.38), channel_id=1, source_target_pairs={{0,64},{8,72},{16,80},{24,88},{32,96},{40,104},{48,112},{56,120},{... | collective-permute-start | bytes 36872 | tf_op jit(solution)/shard_map/ppermute | solution.py:432
  25.0 6.5 %collective-permute-done = bf16[1,48,128]{2,1,0:T(8,128)(2,1)S(1)} collective-permute-done((bf16[1,48,128]{2,1,0:T(8,128)(2,1)S(1)}, bf16[1,48,128]{2,1,0:T(8,128)(2,1)S(1)}, u32[]{:S(2)}, u32[]{:S(2)}) %collective-permute-start) | collective-permute-done | bytes 12320 | tf_op jit(solution)/shard_map/ppermute | solution.py:432
  31.5 4.0 %collective-permute-start.1 = (bf16[2,48,128]{2,1,0:T(8,128)(2,1)S(1)}, bf16[2,48,128]{2,1,0:T(8,128)(2,1)S(1)}, u32[]{:S(2)}, u32[]{:S(2)}) collective-permute-start(bf16[2,48,128]{2,1,0:T(8,128)(2,1)S(1)} %pad_maximum_fusion.1), channel_id=1, source_target_pairs={{0,32},{8,40},{16,48},{24,56},{32,0},{40,8},{48,16},{56,24},{64,96... | collective-permute-start | bytes 73736 | tf_op jit(solution)/shard_map/ppermute | solution.py:432
  35.5 5.0 %collective-permute-done.1 = bf16[2,48,128]{2,1,0:T(8,128)(2,1)S(1)} collective-permute-done((bf16[2,48,128]{2,1,0:T(8,128)(2,1)S(1)}, bf16[2,48,128]{2,1,0:T(8,128)(2,1)S(1)}, u32[]{:S(2)}, u32[]{:S(2)}) %collective-permute-start.1) | collective-permute-done | bytes 24608 | tf_op jit(solution)/shard_map/ppermute | solution.py:432
  40.5 0.0 all-to-all-done.r_ref
  40.5 0.7 tile.4
  41.2 0.0 copy-done.6
  41.2 3.9 %all-to-all-start.1 = ((bf16[16,48,128]{2,1,0:T(8,128)(2,1)}), bf16[16,48,128]{2,1,0:T(8,128)(2,1)S(1)}, u32[]{:S(2)}, u32[]{:S(2)}) async-start(bf16[16,48,128]{2,1,0:T(8,128)(2,1)} %bitcast), calls=%async_computation.1 | async-start | bytes 393216 | tf_op jit(solution)/shard_map/all_to_all | solution.py:434
  45.1 1.7 %mid.1.m_ref = bf16[8,72,128]{2,1,0:T(8,128)(2,1)S(1)} custom-call(bf16[8,216,128]{2,1,0:T(8,128)(2,1)S(1)} %all-to-all-done.r_ref), custom_call_target="tpu_custom_call" | custom-call | flops 268435456 | bytes 524288 | tf_op jit(solution)/shard_map/mid/pallas_call | solution.py:37
  46.8 3.5 %all-to-all-done.1.others_ref = bf16[16,48,128]{2,1,0:T(8,128)(2,1)S(1)} async-done(((bf16[16,48,128]{2,1,0:T(8,128)(2,1)}), bf16[16,48,128]{2,1,0:T(8,128)(2,1)S(1)}, u32[]{:S(2)}, u32[]{:S(2)}) %all-to-all-start.1) | async-done | bytes 196640 | tf_op jit(solution)/shard_map/all_to_all | solution.py:434
  50.3 1.1 %far.1 = bf16[8,104,128]{2,1,0:T(8,128)(2,1)} custom-call(bf16[8,216,128]{2,1,0:T(8,128)(2,1)S(1)} %all-to-all-done.r_ref, bf16[16,48,128]{2,1,0:T(8,128)(2,1)S(1)} %all-to-all-done.1.others_ref, bf16[8,72,128]{2,1,0:T(8,128)(2,1)S(1)} %mid.1.m_ref), custom_call_target="tpu_custom_call" | custom-call | tf_op jit(solution)/shard_map/far/pallas_call | solution.py:297
  51.4 8.3 %all-to-all-start.2 = ((bf16[8,104,128]{2,1,0:T(8,128)(2,1)}), bf16[8,104,128]{2,1,0:T(8,128)(2,1)S(1)}, u32[]{:S(2)}, u32[]{:S(2)}) async-start(bf16[8,104,128]{2,1,0:T(8,128)(2,1)} %far.1), calls=%async_computation.2 | async-start | bytes 425984 | tf_op jit(solution)/shard_map/all_to_all | solution.py:442
  59.7 0.3 maps.1.refs_7_
  60.0 0.0 copy-start.5
  60.0 0.9 %copy-done.5 = bf16[1024,128]{1,0:T(8,128)(2,1)S(1)} copy-done((bf16[1024,128]{1,0:T(8,128)(2,1)S(1)}, bf16[1024,128]{1,0:T(8,128)(2,1)}, u32[]{:S(2)}) %copy-start.5) | copy-done | bytes 262168
  61.0 0.9 %copy-done.7 = bf16[1024,128]{1,0:T(8,128)(2,1)S(1)} copy-done((bf16[1024,128]{1,0:T(8,128)(2,1)S(1)}, bf16[1024,128]{1,0:T(8,128)(2,1)}, u32[]{:S(2)}) %copy-start.7) | copy-done | bytes 262168
  61.9 3.0 %near.5 = (bf16[128,1024]{1,0:T(8,128)(2,1)S(1)}, f32[1,8,1024]{2,1,0:T(8,128)S(1)}) custom-call(bf16[1024,128]{1,0:T(8,128)(2,1)S(1)} %get-tuple-element.30.q_ref, bf16[1024,128]{1,0:T(8,128)(2,1)S(1)} %copy-done.5, bf16[1024,128]{1,0:T(8,128)(2,1)S(1)} %copy-done.7), custom_call_target="tpu_custom_call" | custom-call | flops 536870912 | bytes 1048576 | tf_op jit(solution)/shard_map/near/pallas_call | solution.py:37
  64.9 0.0 copy-done.1
  64.9 0.0 copy-done.3
  64.9 3.0 %near.4 = (bf16[128,1024]{1,0:T(8,128)(2,1)S(1)}, f32[1,8,1024]{2,1,0:T(8,128)S(1)}) custom-call(bf16[1024,128]{1,0:T(8,128)(2,1)S(1)} %get-tuple-element.26.q_ref, bf16[1024,128]{1,0:T(8,128)(2,1)S(1)} %copy-done.1, bf16[1024,128]{1,0:T(8,128)(2,1)S(1)} %copy-done.3), custom_call_target="tpu_custom_call" | custom-call | flops 536870912 | bytes 1048576 | tf_op jit(solution)/shard_map/near/pallas_call | solution.py:37
  67.9 3.0 %near.3 = (bf16[128,1024]{1,0:T(8,128)(2,1)S(1)}, f32[1,8,1024]{2,1,0:T(8,128)S(1)}) custom-call(bf16[1024,128]{1,0:T(8,128)(2,1)S(1)} %get-tuple-element.22.q_ref, bf16[1024,128]{1,0:T(8,128)(2,1)S(1)} %get-tuple-element.23.k_ref, bf16[1024,128]{1,0:T(8,128)(2,1)S(1)} %get-tuple-element.24.v_ref), custom_call_target="tpu_custom_call" | custom-call | flops 536870912 | bytes 1048576 | tf_op jit(solution)/shard_map/near/pallas_call | solution.py:37
  70.8 0.0 all-to-all-done.2.refs_6_
  70.8 2.0 %merge.1 = bf16[1024,384]{1,0:T(8,128)(2,1)} custom-call(bf16[128,1024]{1,0:T(8,128)(2,1)S(1)} %get-tuple-element.25.refs_0_, bf16[128,1024]{1,0:T(8,128)(2,1)S(1)} %get-tuple-element.29.refs_1_, bf16[128,1024]{1,0:T(8,128)(2,1)S(1)} %get-tuple-element.33.refs_2_, f32[1,8,1024]{2,1,0:T(8,128)S(1)} %get-tuple-element.34.refs_3_, ...), custom_call_target="tpu_custom_call" | custom-call | tf_op jit(solution)/shard_map/merge/pallas_call | solution.py:412
  (5 shorter events, 0.0 us)
Async XLA Ops:
  2.6 0.7 copy-start
  3.3 0.7 copy-start.2
  4.0 0.7 copy-start.4
  4.7 36.5 %copy-start.6 = (bf16[1024,128]{1,0:T(8,128)(2,1)}, bf16[1024,128]{1,0:T(8,128)(2,1)S(1)}, u32[]{:S(2)}) copy-start(bf16[1024,128]{1,0:T(8,128)(2,1)S(1)} %get-tuple-element.32.v_ref) | copy-start | bytes 786436
  4.7 35.8 %all-to-all-start = ((bf16[8,216,128]{2,1,0:T(8,128)(2,1)}), bf16[8,216,128]{2,1,0:T(8,128)(2,1)S(1)}, u32[]{:S(2)}, u32[]{:S(2)}) async-start(bf16[8,216,128]{2,1,0:T(8,128)(2,1)} %get-tuple-element.37), calls=%async_computation | async-start | bytes 884736 | tf_op jit(solution)/shard_map/all_to_all | solution.py:430
  14.9 16.6 %collective-permute-start = (bf16[1,48,128]{2,1,0:T(8,128)(2,1)S(1)}, bf16[1,48,128]{2,1,0:T(8,128)(2,1)S(1)}, u32[]{:S(2)}, u32[]{:S(2)}) collective-permute-start(bf16[1,48,128]{2,1,0:T(8,128)(2,1)S(1)} %get-tuple-element.38), channel_id=1, source_target_pairs={{0,64},{8,72},{16,80},{24,88},{32,96},{40,104},{48,112},{56,120},{... | collective-permute-start | bytes 36872 | tf_op jit(solution)/shard_map/ppermute | solution.py:432
  31.5 9.0 %collective-permute-start.1 = (bf16[2,48,128]{2,1,0:T(8,128)(2,1)S(1)}, bf16[2,48,128]{2,1,0:T(8,128)(2,1)S(1)}, u32[]{:S(2)}, u32[]{:S(2)}) collective-permute-start(bf16[2,48,128]{2,1,0:T(8,128)(2,1)S(1)} %pad_maximum_fusion.1), channel_id=1, source_target_pairs={{0,32},{8,40},{16,48},{24,56},{32,0},{40,8},{48,16},{56,24},{64,96... | collective-permute-start | bytes 73736 | tf_op jit(solution)/shard_map/ppermute | solution.py:432
  41.2 9.1 %all-to-all-start.1 = ((bf16[16,48,128]{2,1,0:T(8,128)(2,1)}), bf16[16,48,128]{2,1,0:T(8,128)(2,1)S(1)}, u32[]{:S(2)}, u32[]{:S(2)}) async-start(bf16[16,48,128]{2,1,0:T(8,128)(2,1)} %bitcast), calls=%async_computation.1 | async-start | bytes 393216 | tf_op jit(solution)/shard_map/all_to_all | solution.py:434
  51.4 19.4 %all-to-all-start.2 = ((bf16[8,104,128]{2,1,0:T(8,128)(2,1)}), bf16[8,104,128]{2,1,0:T(8,128)(2,1)S(1)}, u32[]{:S(2)}, u32[]{:S(2)}) async-start(bf16[8,104,128]{2,1,0:T(8,128)(2,1)} %far.1), calls=%async_computation.2 | async-start | bytes 425984 | tf_op jit(solution)/shard_map/all_to_all | solution.py:442
  60.0 1.0 %copy-start.5 = (bf16[1024,128]{1,0:T(8,128)(2,1)S(1)}, bf16[1024,128]{1,0:T(8,128)(2,1)}, u32[]{:S(2)}) copy-start(bf16[1024,128]{1,0:T(8,128)(2,1)} %copy-done.4) | copy-start | bytes 786436
  61.0 0.9 %copy-start.7 = (bf16[1024,128]{1,0:T(8,128)(2,1)S(1)}, bf16[1024,128]{1,0:T(8,128)(2,1)}, u32[]{:S(2)}) copy-start(bf16[1024,128]{1,0:T(8,128)(2,1)} %copy-done.6) | copy-start | bytes 786436
  61.9 3.0 %copy-start.1 = (bf16[1024,128]{1,0:T(8,128)(2,1)S(1)}, bf16[1024,128]{1,0:T(8,128)(2,1)}, u32[]{:S(2)}) copy-start(bf16[1024,128]{1,0:T(8,128)(2,1)} %copy-done) | copy-start | bytes 786436
  61.9 3.0 %copy-start.3 = (bf16[1024,128]{1,0:T(8,128)(2,1)S(1)}, bf16[1024,128]{1,0:T(8,128)(2,1)}, u32[]{:S(2)}) copy-start(bf16[1024,128]{1,0:T(8,128)(2,1)} %copy-done.2) | copy-start | bytes 786436
